TPU v7x, 32 devices: a whole 2x2x4 slice. The times are simulated.
32 devices in a mesh: field: 2 (over core), dom: 16 (over z, y, x).
Axes of the slice: x: 2, y: 2, z: 4, core: 2. Of those that a mesh axis runs over, the one named last changes fastest.
Arguments:
- modes: float32 [2, 40, 131072], P('field', None, 'dom'), may hold values from -6 to 6
- previous: float32 [2, 40, 131072], P('field', None, 'dom'), may hold values from -6 to 6
- kinds: int32 [2, 3, 256], P('field'), may hold values from 0 to 3
- scales: float32 [2, 3, 256], P('field'), may hold values from 0.5 to 4
- tables: bfloat16 [2, 3, 4, 512, 512], P('field'), may hold values from -2 to 6, as said below
- wet_rows: int32 [2, 49152], P('field', 'dom'), may hold values from 0 to 8191, as said below
- wet_counts: int32 [16], P('dom'), may hold values from 768 to 3072, as said below
- coupling: float32 [49152], P('dom'), may hold values from -6 to 6
Outputs:
- basis: float32 [2, 120, 131072], P('field', None, 'dom')
- projected: float32 [120, 120], replicated
Inputs may be any that keep to these rules, and one draw needn't show every extreme that they name: `tables`: tables of offset 0 are symmetric. `wet_rows`: within each subdomain and field the 3072 row numbers are distinct. `wet_counts`: some subdomain uses all 3072 slots.
All inputs are finite; a program needn't handle non-finite values.
Results may differ from a plain program's by a relative error of at most 0.00045.
The roundings to bfloat16 on the way count: a program that leaves them out, or rounds other values in their place, can miss the bound.
Values may be sent and summed in bfloat16 or wider, within the bound.
A program may use at most 192 MiB of HBM per device.

v0:
```python
import jax
import jax.numpy as jnp
from jax import lax
from jax.sharding import PartitionSpec as P

BS = 512
NTYPE = 4
NBR = 16
IFACE = 3072


def for_sending(shard):
    return jax.tree.map(lambda a: a.astype(jnp.bfloat16) if a.dtype == jnp.float32 else a, shard)


def swapped(shard, axis, apart):
    return lax.ppermute(shard, axis, [(i, i ^ 1 << apart) for i in range(lax.axis_size(axis))])


def extended(cells, sides, width):
    for axis, dim in sides:
        count = lax.axis_size(axis)
        ends = count - 1
        head = lax.slice_in_dim(cells, 0, width, axis=dim)
        tail = lax.slice_in_dim(cells, cells.shape[dim] - width, cells.shape[dim], axis=dim)
        cells = jnp.concatenate(
            [
                lax.ppermute(tail, axis, [(i, (i + 1) % count) for i in range(ends)]),
                cells,
                lax.ppermute(head, axis, [((i + 1) % count, i) for i in range(ends)]),
            ],
            axis=dim,
        )
    return cells


def typed_product(blocks, table_set, type_ids, factors, transposed):
    columns = blocks.shape[0]
    count = blocks.shape[1]
    flattened = blocks.reshape(columns * count, BS)
    contract = 0 if transposed else 1
    result = jnp.zeros((columns, count, BS), jnp.float32)
    for type_id in range(NTYPE):
        product = lax.dot_general(
            flattened,
            table_set[type_id],
            (((1,), (contract,)), ((), ())),
            preferred_element_type=jnp.float32,
        )
        factor_t = jnp.where(type_ids == type_id, factors, jnp.float32(0.0))
        result = result + factor_t[None, :, None] * product.reshape(columns, count, BS)
    return result


def block_product(window, kinds, scales, tables):
    columns = window.shape[0]
    blocks = window.reshape(columns, NBR + 4, BS)
    result = typed_product(blocks[:, 2 : NBR + 2], tables[0], kinds[0, 2:], scales[0, 2:], False)
    for offset in (1, 2):
        result = result + typed_product(
            blocks[:, 2 + offset : NBR + 2 + offset],
            tables[offset],
            kinds[offset, 2:],
            scales[offset, 2:],
            False,
        )
        result = result + typed_product(
            blocks[:, 2 - offset : NBR + 2 - offset],
            tables[offset],
            kinds[offset, 2 - offset : NBR + 2 - offset],
            scales[offset, 2 - offset : NBR + 2 - offset],
            True,
        )
    return result.reshape(columns, NBR * BS)


def operate(window, vectors, kinds, scales, tables, rows, weights):
    images = block_product(window, kinds, scales, tables)
    values = jnp.take(vectors, rows, axis=1) * weights[None, :]
    received = swapped(for_sending(values), "field", 0).astype(values.dtype)
    return images.at[:, rows].add(received)


def shards(modes, previous, kinds, scales, tables, wet_rows, wet_counts, coupling):
    highest = lax.Precision.HIGHEST
    domain = lax.axis_index("dom")
    vec_modes = modes[0]
    vec_prev = previous[0]
    field_tables = tables[0]
    kinds_pad = jnp.pad(kinds[0], ((0, 0), (2, 0)))
    scales_pad = jnp.pad(scales[0], ((0, 0), (2, 0)))
    local_kinds = lax.dynamic_slice_in_dim(kinds_pad, domain * NBR, NBR + 2, 1)
    local_scales = lax.dynamic_slice_in_dim(scales_pad, domain * NBR, NBR + 2, 1)
    rows = wet_rows[0]
    used = jnp.arange(IFACE, dtype=jnp.int32) < wet_counts[0]
    weights = jnp.where(used, coupling, jnp.float32(0.0))
    window_modes = extended(vec_modes.astype(jnp.bfloat16), (("dom", 1),), 2 * BS)
    image_x = operate(
        window_modes, vec_modes, local_kinds, local_scales, field_tables, rows, weights
    )
    squares, products = lax.psum(
        (jnp.sum(vec_modes * vec_modes, axis=1), jnp.sum(vec_modes * image_x, axis=1)),
        ("field", "dom"),
    )
    quotient = products / squares
    diag_table = jnp.diagonal(field_tables[0], axis1=1, axis2=2).astype(jnp.float32)
    selector = (local_kinds[0, 2:][:, None] == jnp.arange(NTYPE, dtype=jnp.int32)[None, :]).astype(
        jnp.float32
    )
    row_diag = jnp.dot(selector, diag_table, precision=highest)
    jacobi = (local_scales[0, 2:][:, None] * row_diag).reshape(NBR * BS)
    residual_dir = (image_x - vec_modes * quotient[:, None]) / jacobi[None, :]
    pair = jnp.concatenate([residual_dir, vec_prev], axis=0)
    window_pair = extended(pair.astype(jnp.bfloat16), (("dom", 1),), 2 * BS)
    image_wp = operate(window_pair, pair, local_kinds, local_scales, field_tables, rows, weights)
    search = jnp.concatenate([vec_modes, pair], axis=0)
    image_all = jnp.concatenate([image_x, image_wp], axis=0)
    ndof = 2.0 * lax.axis_size("dom") * NBR * BS
    summed_b, summed_a = lax.psum(
        (
            jnp.dot(search, search.T, precision=highest),
            jnp.dot(search, image_all.T, precision=highest),
        ),
        ("field", "dom"),
    )
    gram_b = summed_b / ndof
    gram_a = (summed_a + summed_a.T) / (2.0 * ndof)
    chol = jnp.linalg.cholesky(gram_b)
    leading = jax.scipy.linalg.solve_triangular(chol, gram_a, lower=True)
    projected = jax.scipy.linalg.solve_triangular(chol, leading.T, lower=True)
    basis = jax.scipy.linalg.solve_triangular(chol, search, lower=True)
    return (basis[None], projected)


def solution(mesh):
    return jax.shard_map(
        shards,
        mesh=mesh,
        in_specs=(
            P("field", None, "dom"),
            P("field", None, "dom"),
            P("field", None, None),
            P("field", None, None),
            P("field", None, None, None, None),
            P("field", "dom"),
            P("dom"),
            P("dom"),
        ),
        out_specs=(P("field", None, "dom"), P()),
        check_vma=False,
    )
```

profile of v0, /device:TPU:0, one launch (start us, length us, event | category | flops | bytes accessed | tf_op | source)
XLA Modules:
  0.0 542.5 jit_solution(1693732785863256557)
XLA Ops:
  7.2 3.7 copy.30
  14.2 5.6 %collective-permute-start = (bf16[40,1024]{0,1:T(8,128)(2,1)}, bf16[40,1024]{0,1:T(8,128)(2,1)}, u32[]{:S(2)}, u32[]{:S(2)}) collective-permute-start(bf16[40,1024]{0,1:T(8,128)(2,1)} %get-tuple-element.18), channel_id=1, source_target_pairs={{0,1},{1,2},{2,3},{3,4},{4,5},{5,6},{6,7},{7,8},{8,9},{9,10},{10,1... | collective-permute-start | bytes 245768 | tf_op jit(solution)/shard_map/ppermute | solution.py:28
  21.7 13.1 %gather_fusion = f32[3072,40]{1,0:T(8,128)} fusion(f32[40,8192]{0,1:T(8,128)} %bitcast.254, s32[3072]{0:T(1024)S(1)} %broadcast_clamp_fusion), kind=kCustom, calls=%fused_computation | custom fusion | bytes 995328 | tf_op jit(solution)/shard_map/jit(_take)/gather | solution.py:79
  41.7 41.6 %copy.52 = bf16[1,1,4,512,512]{2,4,3,1,0:T(8,128)(2,1)} copy(bf16[1,1,4,512,512]{4,3,2,1,0:T(8,128)(2,1)S(1)} %slice-done.8) | data formatting | bytes 4194304
  83.3 6.5 %gather_fusion.1 = bf16[512,4]{1,0:T(8,128)(2,1)S(1)} fusion(bf16[4,512,512]{0,2,1:T(8,128)(2,1)} %bitcast.58, s32[512]{0:T(512)S(1)} %bitcast.269), kind=kCustom, calls=%fused_computation.1 | custom fusion | bytes 12288 | tf_op jit(solution)/shard_map/jit(diagonal)/gather | solution.py:106
  90.0 3.9 copy.38
  116.3 19.6 %scatter_fusion = f32[40,8192]{0,1:T(8,128)} fusion(f32[40,8192]{0,1:T(8,128)} %bitcast.256, s32[3072]{0:T(1024)S(1)} %bitcast.271, f32[3072,40]{1,0:T(8,128)S(1)} %copy.36), kind=kCustom, calls=%fused_computation.3 | custom fusion | flops 122880 | bytes 1486848 | tf_op jit(solution)/shard_map/scatter-add | solution.py:81
  135.9 4.6 multiply_reduce_fusion
  140.4 41.7 %all-reduce.3 = (f32[40]{0:T(128)S(1)}, f32[40]{0:T(128)S(1)}) all-reduce(f32[40]{0:T(128)S(1)} %get-tuple-element.4, f32[40]{0:T(128)S(1)} %get-tuple-element.3), channel_id=1, replica_groups=mesh['field'=2,'dom'=16] {'field','dom'}, use_global_device_ids=true, to_apply=%region_2.3 | all-reduce | flops 80 | bytes 640 | tf_op jit(solution)/shard_map/psum | solution.py:101
  182.2 6.0 %subtract_divide_fusion = f32[40,8192]{0,1:T(8,128)S(1)} fusion(f32[40,8192]{0,1:T(8,128)} %scatter_fusion, f32[8192]{0:T(1024)S(1)} %bitcast.273, f32[40]{0:T(128)S(1)} %div.33, f32[1,40,8192]{1,2,0:T(8,128)} %copy.30), kind=kLoop, calls=%fused_computation.12 | loop fusion | flops 983040 | bytes 3965088 | tf_op jit(solution)/shard_map/div | solution.py:112
  191.3 4.2 pad_maximum_fusion
  196.4 4.2 collective-permute-start.3
  201.9 13.5 %gather_fusion.2 = f32[3072,80]{1,0:T(8,128)} fusion(f32[80,8192]{0,1:T(8,128)} %get-tuple-element.10, s32[3072]{0:T(1024)S(1)} %broadcast_clamp_fusion), kind=kCustom, calls=%fused_computation.2 | custom fusion | bytes 1978368 | tf_op jit(solution)/shard_map/jit(_take)/gather | solution.py:79
  219.3 10.8 %fusion.178 = f32[120,120]{0,1:T(8,128)} fusion(f32[120,8192]{0,1:T(8,128)} %pad_maximum_fusion), kind=kOutput, calls=%fused_computation.259 | convolution fusion | flops 1415577600 | bytes 3989760 | tf_op jit(solution)/shard_map/dot_general | solution.py:121
  230.1 7.7 %pad_maximum_fusion.2 = bf16[80,10240]{0,1:T(8,128)(2,1)S(1)} fusion(bf16[80,1024]{0,1:T(8,128)(2,1)S(1)} %collective-permute-done.4, bf16[80,8192]{0,1:T(8,128)(2,1)S(1)} %get-tuple-element.9, bf16[80,1024]{0,1:T(8,128)(2,1)S(1)} %collective-permute-done.3), kind=kLoop, calls=%fused_computation.15 | loop fusion | flops 4915200 | bytes 3276800 | tf_op jit(solution)/shard_map/concatenate | solution.py:26
  237.8 4.2 fusion.175
  245.3 3.6 fusion.26
  260.0 3.8 fusion.39
  263.8 3.6 fusion.45
  270.5 3.5 fusion.43
  292.1 3.9 fusion.67
  296.0 4.4 copy.54
  300.5 4.0 fusion.63
  304.5 4.0 fusion.69
  317.9 19.0 %add_add_fusion = f32[80,16,512]{2,1,0:T(8,128)} fusion(f32[80,16,512]{2,1,0:T(8,128)} %fusion.43, f32[80,16,512]{2,1,0:T(8,128)} %fusion.49, f32[80,16,512]{2,1,0:T(8,128)} %fusion.55, f32[80,16,512]{2,1,0:T(8,128)} %fusion.39, f32[80,16,512]{2,1,0:T(8,128)} %fusion.45, f32[80,16,512]{2,1,0:T(8,128)} %fusion.51, f32[80,16,512]{2,1,0:T(8,128)} %fusion.57, ...), kind=kOutput, calls=%fused_computation.16 | convolution fusion | flops 696647680 | bytes 54265088 | tf_op jit(solution)/shard_map/dot_general | solution.py:44
  336.9 4.9 copy.49
  343.4 19.6 %scatter_fusion.1 = f32[80,8192]{0,1:T(8,128)} fusion(f32[80,8192]{0,1:T(8,128)} %bitcast.258, s32[3072]{0:T(1024)S(1)} %bitcast.272, f32[3072,80]{1,0:T(8,128)S(1)} %copy.44), kind=kCustom, calls=%fused_computation.4 | custom fusion | flops 245760 | bytes 2961408 | tf_op jit(solution)/shard_map/scatter-add | solution.py:81
  363.0 13.1 %fusion = f32[120,120]{1,0:T(8,128)} fusion(f32[120,8192]{0,1:T(8,128)} %pad_maximum_fusion, f32[80,8192]{0,1:T(8,128)} %scatter_fusion.1, f32[40,8192]{0,1:T(8,128)} %scatter_fusion), kind=kOutput, calls=%fused_computation.8 | convolution fusion | flops 1416560640 | bytes 7921920 | tf_op jit(solution)/shard_map/dot_general | solution.py:122
  376.2 125.3 %all-reduce.6.cloned.1.call-done = (f32[120,120]{0,1:T(8,128)}, f32[120,120]{1,0:T(8,128)}) async-done(((f32[120,120]{0,1:T(8,128)}, f32[120,120]{1,0:T(8,128)}), (f32[120,120]{0,1:T(8,128)}, f32[120,120]{1,0:T(8,128)})) %all-reduce.6.cloned.1.call-update) | async-done | bytes 115216 | tf_op jit(solution)/shard_map/psum | solution.py:119
  503.3 11.0 %cholesky.16 = f32[120,120]{1,0:T(8,128)S(1)} custom-call(f32[120,120]{1,0:T(8,128)S(1)} %fusion.152), custom_call_target="Cholesky" | custom-call | tf_op jit(solution)/shard_map/jit(cholesky)/cholesky | solution.py:128
  515.6 9.5 %custom-call.10 = f32[1,120,120]{1,2,0:T(8,128)S(1)} custom-call(f32[1,120,120]{2,1,0:T(8,128)S(1)} %fusion.145), custom_call_target="InvertDiagBlocksLowerTriangular" | custom-call | tf_op jit(solution)/shard_map/jit(_solve_triangular)/triangular_solve | solution.py:131
  526.0 7.9 %convolution_bitcast_fusion = f32[1,120,8192]{2,1,0:T(8,128)} fusion(f32[120,8192]{0,1:T(8,128)} %pad_maximum_fusion, f32[1,120,120]{1,2,0:T(8,128)S(1)} %custom-call.10), kind=kOutput, calls=%fused_computation.5 | convolution fusion | flops 1415577600 | bytes 7921920 | tf_op jit(solution)/shard_map/jit(_solve_triangular)/triangular_solve | solution.py:131
  (139 shorter events, 94.8 us)
Async XLA Ops:
  7.2 494.4 %all-reduce.6.cloned.1.call-start = ((), (), s32[]{:S(2)}) async-start(), calls=%async_computation | async-start | bytes 245760 | tf_op jit(solution)/shard_map/psum | solution.py:119
  10.9 10.1 %copy-start.9 = (s32[1,3072]{1,0:T(1,128)S(1)}, s32[1,3072]{1,0:T(1,128)}, u32[]{:S(2)}) copy-start(s32[1,3072]{1,0:T(1,128)} %param.15) | copy-start | bytes 36868
  13.3 21.5 %copy-start.10 = (f32[3072]{0:T(1024)S(1)}, f32[3072]{0:T(1024)}, u32[]{:S(2)}) copy-start(f32[3072]{0:T(1024)} %param.17) | copy-start | bytes 36868
  14.2 79.7 %collective-permute-start = (bf16[40,1024]{0,1:T(8,128)(2,1)}, bf16[40,1024]{0,1:T(8,128)(2,1)}, u32[]{:S(2)}, u32[]{:S(2)}) collective-permute-start(bf16[40,1024]{0,1:T(8,128)(2,1)} %get-tuple-element.18), channel_id=1, source_target_pairs={{0,1},{1,2},{2,3},{3,4},{4,5},{5,6},{6,7},{7,8},{8,9},{9,10},{10,1... | collective-permute-start | bytes 245768 | tf_op jit(solution)/shard_map/ppermute | solution.py:28
  19.7 75.2 %collective-permute-start.1 = (bf16[40,1024]{0,1:T(8,128)(2,1)}, bf16[40,1024]{0,1:T(8,128)(2,1)S(1)}, u32[]{:S(2)}, u32[]{:S(2)}) collective-permute-start(bf16[40,1024]{0,1:T(8,128)(2,1)} %get-tuple-element.19), channel_id=1, source_target_pairs={{1,0},{2,1},{3,2},{4,3},{5,4},{6,5},{7,6},{8,7},{9,8},{10,9},{11,1... | collective-permute-start | bytes 245768 | tf_op jit(solution)/shard_map/ppermute | solution.py:30
  34.8 5.3 copy-start.11
  34.8 5.3 copy-start.12
  38.6 76.2 %collective-permute-start.2 = (bf16[40,3072]{1,0:T(8,128)(2,1)}, bf16[40,3072]{1,0:T(8,128)(2,1)}, u32[]{:S(2)}, u32[]{:S(2)}) collective-permute-start(bf16[40,3072]{1,0:T(8,128)(2,1)} %copy.34), channel_id=1, source_target_pairs={{0,16},{16,0},{1,17},{17,1},{2,18},{18,2},{3,19},{19,3},{4,20},{20... | collective-permute-start | bytes 737288 | tf_op jit(solution)/shard_map/ppermute | solution.py:17
  40.1 1.6 slice-start.8
  90.0 5.1 copy-start.7
  95.7 8.2 %slice-start = ((s8[6291456]{0:T(1024)(128)(4,1)}), s8[4194304]{0:T(1024)(128)(4,1)S(1)}, s32[]{:S(2)}) async-start(s8[6291456]{0:T(1024)(128)(4,1)} %bitcast.259), calls=%async_computation.1 | async-start | bytes 8388608
  99.0 4.9 slice-start.1
  182.1 6.0 %copy-start.1 = (f32[1,40,8192]{1,2,0:T(8,128)S(1)}, f32[1,40,8192]{1,2,0:T(8,128)}, u32[]{:S(2)}) copy-start(f32[1,40,8192]{1,2,0:T(8,128)} %copy.38) | copy-start | bytes 3932164
  188.2 3.2 copy-start
  196.4 33.7 %collective-permute-start.3 = (bf16[80,1024]{0,1:T(8,128)(2,1)}, bf16[80,1024]{0,1:T(8,128)(2,1)S(1)}, u32[]{:S(2)}, u32[]{:S(2)}) collective-permute-start(bf16[80,1024]{0,1:T(8,128)(2,1)} %get-tuple-element.16), channel_id=1, source_target_pairs={{0,1},{1,2},{2,3},{3,4},{4,5},{5,6},{6,7},{7,8},{8,9},{9,10},{10,1... | collective-permute-start | bytes 491528 | tf_op jit(solution)/shard_map/ppermute | solution.py:28
  200.6 29.5 %collective-permute-start.4 = (bf16[80,1024]{0,1:T(8,128)(2,1)}, bf16[80,1024]{0,1:T(8,128)(2,1)S(1)}, u32[]{:S(2)}, u32[]{:S(2)}) collective-permute-start(bf16[80,1024]{0,1:T(8,128)(2,1)} %get-tuple-element.17), channel_id=1, source_target_pairs={{1,0},{2,1},{3,2},{4,3},{5,4},{6,5},{7,6},{8,7},{9,8},{10,9},{11,1... | collective-permute-start | bytes 491528 | tf_op jit(solution)/shard_map/ppermute | solution.py:30
  219.3 122.5 %collective-permute-start.5 = (bf16[80,3072]{1,0:T(8,128)(2,1)}, bf16[80,3072]{1,0:T(8,128)(2,1)}, u32[]{:S(2)}, u32[]{:S(2)}) collective-permute-start(bf16[80,3072]{1,0:T(8,128)(2,1)} %copy.42), channel_id=1, source_target_pairs={{0,16},{16,0},{1,17},{17,1},{2,18},{18,2},{3,19},{19,3},{4,20},{20... | collective-permute-start | bytes 1474568 | tf_op jit(solution)/shard_map/ppermute | solution.py:17
  242.0 10.2 %slice-start.2 = ((s8[6291456]{0:T(1024)(128)(4,1)}), s8[2097152]{0:T(1024)(128)(4,1)S(1)}, s32[]{:S(2)}) async-start(s8[6291456]{0:T(1024)(128)(4,1)} %bitcast.261), calls=%async_computation.3 | async-start | bytes 4194304
  245.2 7.0 %slice-start.3 = ((s8[6291456]{0:T(1024)(128)(4,1)}), s8[4194304]{0:T(1024)(128)(4,1)S(1)}, s32[]{:S(2)}) async-start(s8[6291456]{0:T(1024)(128)(4,1)} %bitcast.261), calls=%async_computation.4 | async-start | bytes 8388608
  260.0 7.4 %copy-start.4 = (bf16[80,16,512]{2,1,0:T(8,128)(2,1)}, bf16[80,16,512]{2,1,0:T(8,128)(2,1)S(1)}, u32[]{:S(2)}) copy-start(bf16[80,16,512]{2,1,0:T(8,128)(2,1)S(1)} %copy.56) | copy-start | bytes 3932164
  263.8 13.7 %slice-start.4 = ((s8[6291456]{0:T(1024)(128)(4,1)}), s8[2097152]{0:T(1024)(128)(4,1)S(1)}, s32[]{:S(2)}) async-start(s8[6291456]{0:T(1024)(128)(4,1)} %bitcast.263), calls=%async_computation.5 | async-start | bytes 4194304
  270.5 7.0 %slice-start.5 = ((s8[6291456]{0:T(1024)(128)(4,1)}), s8[4194304]{0:T(1024)(128)(4,1)S(1)}, s32[]{:S(2)}) async-start(s8[6291456]{0:T(1024)(128)(4,1)} %bitcast.263), calls=%async_computation.6 | async-start | bytes 8388608
  274.0 3.5 copy-start.5
  287.7 1.1 copy-start.2
  292.1 16.3 %slice-start.6 = ((s8[6291456]{0:T(1024)(128)(4,1)}), s8[2097152]{0:T(1024)(128)(4,1)S(1)}, s32[]{:S(2)}) async-start(s8[6291456]{0:T(1024)(128)(4,1)} %bitcast.265), calls=%async_computation.7 | async-start | bytes 4194304
  300.5 8.0 %slice-start.7 = ((s8[6291456]{0:T(1024)(128)(4,1)}), s8[4194304]{0:T(1024)(128)(4,1)S(1)}, s32[]{:S(2)}) async-start(s8[6291456]{0:T(1024)(128)(4,1)} %bitcast.265), calls=%async_computation.8 | async-start | bytes 8388608
  304.5 4.0 copy-start.3
  308.4 2.3 copy-start.6
  526.0 7.9 %copy-start.8 = (f32[120,120]{1,0:T(8,128)S(1)}, f32[120,120]{1,0:T(8,128)}, u32[]{:S(2)}) copy-start(f32[120,120]{1,0:T(8,128)} %get-tuple-element.6) | copy-start | bytes 172804
Sparse Core Ops, SparseCore 0:
  376.3 125.1 all-reduce.5
where the time goes:
time: 547 us; the launch traced here: 543 us
  matrix products  126 us (23%)
  waiting for transfers between devices  125 us (23%)
  local copies, waits for them, and re-layouts  122 us (22%)
  other arithmetic  98.6 us (18%)
  blocking collectives  41.7 us (8%)
  between operations  15.8 us (3%)
  starting transfers between devices  12.4 us (2%)
    psum x1, waiting for transfers between devices, shards(): lax.psum((jnp.dot(search, search.T, precision=highest), jnp.dot(search, i...  125 us
    dot_general x40, matrix products, typed_product(): lax.dot_general(flattened, table_set[type_id], (((1,), (contract,)), ((),...  93 us
    unnamed x53, local copies, waits for them, and re-layouts  67.2 us
    psum x1, blocking collectives, shards(): lax.psum((jnp.sum(vec_modes * vec_modes, axis=1), jnp.sum(vec_modes * ima...  41.7 us
    scatter-add x2, other arithmetic, operate(): return images.at[:, rows].add(received)  39.2 us
    gather x2, local copies, waits for them, and re-layouts, operate(): values = jnp.take(vectors, rows, axis=1) * weights[None, :]  26.6 us
    dot_general x1, matrix products, shards(): jnp.dot(search, image_all.T, precision=highest)  13.1 us
    another operation x3, other arithmetic, shards(): chol = jnp.linalg.cholesky(gram_b)  11.6 us
  transfers between devices with their start and end apart: 7, of which 1 were waited for; matrix products, arithmetic and copies ran while one was open for 42% of the time, Pallas kernels for 0%

commit v1 on v0

v1 whole, which is shorter than its diff:
```python
import functools

import jax
import jax.numpy as jnp
from jax import lax
from jax.experimental import pallas as pl
from jax.experimental.pallas import tpu as pltpu
from jax.sharding import PartitionSpec as P

BS = 512


def for_sending(shard):
    return jax.tree.map(lambda a: a.astype(jnp.bfloat16) if a.dtype == jnp.float32 else a, shard)


def swapped(shard, axis, apart):
    return lax.ppermute(shard, axis, [(i, i ^ 1 << apart) for i in range(lax.axis_size(axis))])


def halos(cells, axis, dim, width):
    count = lax.axis_size(axis)
    ends = count - 1
    head = lax.slice_in_dim(cells, 0, width, axis=dim)
    tail = lax.slice_in_dim(cells, cells.shape[dim] - width, cells.shape[dim], axis=dim)
    return (
        lax.ppermute(tail, axis, [(i, i + 1) for i in range(ends)]),
        lax.ppermute(head, axis, [(i + 1, i) for i in range(ends)]),
    )


def doubling_kernel(bits, x_ref, o_ref, held, landed, send_sem, recv_sem):
    field = lax.axis_index("field")
    dom = lax.axis_index("dom")
    partners = [(1 - field, dom)]
    for bit in range(bits):
        step = 1 << bit
        partners.append((field, dom + (1 - 2 * ((dom // step) % 2)) * step))
    barrier = pltpu.get_barrier_semaphore()
    for partner in partners:
        pl.semaphore_signal(
            barrier, inc=1, device_id=partner, device_id_type=pl.DeviceIdType.MESH
        )
    held[0] = x_ref[...]
    pl.semaphore_wait(barrier, len(partners))
    for step, partner in enumerate(partners):
        copy = pltpu.make_async_remote_copy(
            src_ref=held.at[step],
            dst_ref=landed.at[step],
            send_sem=send_sem.at[step],
            recv_sem=recv_sem.at[step],
            device_id=partner,
            device_id_type=pl.DeviceIdType.MESH,
        )
        copy.start()
        copy.wait()
        total = held[step] + landed[step]
        if step + 1 < len(partners):
            held[step + 1] = total
        else:
            o_ref[...] = total


def summed_everywhere(x, collective_id):
    bits = (lax.axis_size("dom") - 1).bit_length()
    steps = bits + 1
    return pl.pallas_call(
        functools.partial(doubling_kernel, bits),
        out_shape=jax.ShapeDtypeStruct(x.shape, x.dtype),
        in_specs=[pl.BlockSpec(memory_space=pltpu.VMEM)],
        out_specs=pl.BlockSpec(memory_space=pltpu.VMEM),
        scratch_shapes=[
            pltpu.VMEM((steps,) + x.shape, x.dtype),
            pltpu.VMEM((steps,) + x.shape, x.dtype),
            pltpu.SemaphoreType.DMA((steps,)),
            pltpu.SemaphoreType.DMA((steps,)),
        ],
        compiler_params=pltpu.CompilerParams(
            collective_id=collective_id, has_side_effects=True
        ),
    )(x)


NN = (((1,), (0,)), ((), ()))
NT = (((1,), (1,)), ((), ()))


def stencil_kernel(kinds, scales, x_ref, before, after, tables, o_ref, window):
    nbr = x_ref.shape[1] // BS
    wide = x_ref.shape[1]
    window[:, : 2 * BS] = before[...]
    window[:, 2 * BS : 2 * BS + wide] = x_ref[...].astype(jnp.bfloat16)
    window[:, 2 * BS + wide :] = after[...]

    def term(n, shift, offset, at, dims):
        block = window[:, pl.ds(pl.multiple_of((n + 2 + shift) * BS, BS), BS)]
        product = lax.dot_general(
            block, tables[offset, kinds[offset, at]], dims, preferred_element_type=jnp.float32
        )
        return scales[offset, at] * product

    def step(n, carry):
        total = term(n, 0, 0, n + 2, NN)
        for offset in (1, 2):
            total = total + term(n, offset, offset, n + 2, NT)
            total = total + term(n, -offset, offset, n + 2 - offset, NN)
        o_ref[:, pl.ds(pl.multiple_of(n * BS, BS), BS)] = total
        return carry

    lax.fori_loop(0, nbr, step, 0)


def block_product(vectors, sides, kinds, scales, tables):
    columns, wide = vectors.shape
    smem = pl.BlockSpec(memory_space=pltpu.SMEM)
    vmem = pl.BlockSpec(memory_space=pltpu.VMEM)
    return pl.pallas_call(
        stencil_kernel,
        out_shape=jax.ShapeDtypeStruct((columns, wide), jnp.float32),
        in_specs=[smem, smem, vmem, vmem, vmem, vmem],
        out_specs=vmem,
        scratch_shapes=[pltpu.VMEM((columns, wide + 4 * BS), jnp.bfloat16)],
        cost_estimate=pl.CostEstimate(
            flops=10 * columns * wide * BS, bytes_accessed=16 * columns * wide, transcendentals=0
        ),
        compiler_params=pltpu.CompilerParams(vmem_limit_bytes=30 * 1024 * 1024),
    )(kinds, scales, vectors, *sides, tables)


def operate(vectors, kinds, scales, tables, rows, weights):
    sides = halos(vectors.astype(jnp.bfloat16), "dom", 1, 2 * BS)
    values = jnp.take(vectors, rows, axis=1) * weights[None, :]
    received = swapped(for_sending(values), "field", 0).astype(values.dtype)
    images = block_product(vectors, sides, kinds, scales, tables)
    return images.at[:, rows].add(received)


def shards(modes, previous, kinds, scales, tables, wet_rows, wet_counts, coupling):
    high = lax.Precision.HIGH
    domain = lax.axis_index("dom")
    vec_modes = modes[0]
    vec_prev = previous[0]
    columns, wide = vec_modes.shape
    nbr = wide // BS
    field_tables = tables[0]
    types = field_tables.shape[1]
    kinds_pad = jnp.pad(kinds[0], ((0, 0), (2, 0)))
    scales_pad = jnp.pad(scales[0], ((0, 0), (2, 0)))
    local_kinds = lax.dynamic_slice_in_dim(kinds_pad, domain * nbr, nbr + 2, 1)
    local_scales = lax.dynamic_slice_in_dim(scales_pad, domain * nbr, nbr + 2, 1)
    rows = wet_rows[0]
    slots = coupling.shape[0]
    used = jnp.arange(slots, dtype=jnp.int32) < wet_counts[0]
    weights = jnp.where(used, coupling, jnp.float32(0.0))
    operands = (local_kinds, local_scales, field_tables, rows, weights)
    first_pair = jnp.concatenate([vec_modes, vec_prev], axis=0)
    image_pair = operate(first_pair, *operands)
    image_x, image_p = image_pair[:columns], image_pair[columns:]
    partial_sums = jnp.stack(
        [jnp.sum(vec_modes * vec_modes, axis=1), jnp.sum(vec_modes * image_x, axis=1)]
    )
    sums = summed_everywhere(jnp.pad(partial_sums, ((0, 6), (0, 128 - columns))), 1)
    quotient = sums[1, :columns] / sums[0, :columns]
    eye = jnp.eye(BS, dtype=jnp.bool_)
    diag_table = jnp.sum(
        jnp.where(eye[None], field_tables[0].astype(jnp.float32), jnp.float32(0.0)), axis=1
    )
    row_diag = jnp.zeros((nbr, BS), jnp.float32)
    for type_id in range(types):
        row_diag = jnp.where(
            (local_kinds[0, 2:] == type_id)[:, None], diag_table[type_id][None, :], row_diag
        )
    jacobi = (local_scales[0, 2:][:, None] * row_diag).reshape(wide)
    residual_dir = (image_x - vec_modes * quotient[:, None]) / jacobi[None, :]
    image_r = operate(residual_dir, *operands)
    search = jnp.concatenate([vec_modes, residual_dir, vec_prev], axis=0)
    image_all = jnp.concatenate([image_x, image_r, image_p], axis=0)
    ndof = 2.0 * lax.axis_size("dom") * wide
    part_b = jnp.dot(search, search.T, precision=high)
    part_a = jnp.dot(search, image_all.T, precision=high)
    part_a = part_a + part_a.T
    size = 3 * columns
    row = lax.broadcasted_iota(jnp.int32, (size, size + 8), 0)
    col = lax.broadcasted_iota(jnp.int32, (size, size + 8), 1)
    packed = jnp.where(
        col <= row,
        jnp.pad(part_b, ((0, 0), (0, 8))),
        jnp.pad(part_a, ((0, 0), (1, 7))),
    )
    packed = summed_everywhere(packed, 2)
    low = jnp.where(col <= row, packed, 0.0)[:, :size]
    high_part = packed[:, 1 : size + 1]
    square_row, square_col = row[:, :size], col[:, :size]
    gram_b = jnp.where(square_col <= square_row, low, low.T) / ndof
    gram_a = jnp.where(square_col >= square_row, high_part, high_part.T) / (2.0 * ndof)
    chol = jnp.linalg.cholesky(gram_b, symmetrize_input=False)
    leading = jax.scipy.linalg.solve_triangular(chol, gram_a, lower=True)
    projected = jax.scipy.linalg.solve_triangular(chol, leading.T, lower=True)
    basis = jax.scipy.linalg.solve_triangular(chol, search, lower=True)
    return (basis[None], projected)


def solution(mesh):
    return jax.shard_map(
        shards,
        mesh=mesh,
        in_specs=(
            P("field", None, "dom"),
            P("field", None, "dom"),
            P("field", None, None),
            P("field", None, None),
            P("field", None, None, None, None),
            P("field", "dom"),
            P("dom"),
            P("dom"),
        ),
        out_specs=(P("field", None, "dom"), P()),
        check_vma=False,
    )
```

time: 547 us -> 241 us (0.44)
  waiting for transfers between devices: 125 us -> 0.02 us
  matrix products: 126 us -> 16 us
  Pallas kernels: 0 us -> 62.1 us
  local copies, waits for them, and re-layouts: 122 us -> 71.7 us
  blocking collectives: 41.7 us -> 0 us
  other arithmetic: 98.6 us -> 77.4 us
  between operations: 15.8 us -> 1.78 us
    psum x1 -> x0, waiting for transfers between devices: 125 us -> none  [shards(): lax.psum((jnp.dot(search, search.T, precision=highest), jnp.dot(search, i...]
    dot_general x43 -> x2, matrix products: 117 us -> 7.99 us  [the longest x1 4.35 us: shards(): part_a = jnp.dot(search, image_all.T, precision=high)]
    pallas_call x0 -> x4, Pallas kernels: none -> 62.1 us  [the longest x2 38.3 us: summed_everywhere(): pl.pallas_call(functools.partial(doubling_kernel, bits), out_shape=jax.Sh...]
    unnamed x53 -> x31, local copies, waits for them, and re-layouts: 67.2 us -> 13.8 us
    psum x1 -> x0, blocking collectives: 41.7 us -> none  [shards(): lax.psum((jnp.sum(vec_modes * vec_modes, axis=1), jnp.sum(vec_modes * ima...]
    concatenate x4 -> x1, other arithmetic: 11.9 us -> 0.2 us  [shards(): first_pair = jnp.concatenate([vec_modes, vec_prev], axis=0)]
    reshape x3 -> x0, local copies, waits for them, and re-layouts: 8.09 us -> none  [the longest x2 7.61 us: block_product(): return result.reshape(columns, NBR * BS)]
    pallas_call x0 -> x2, local copies, waits for them, and re-layouts: none -> 7.54 us  [block_product(): pl.pallas_call(stencil_kernel, out_shape=jax.ShapeDtypeStruct((columns, w...]
  transfers between devices with their start and end apart: 7 -> 6, of which waited for: 1 -> 0; matrix products, arithmetic and copies ran while one was open for 42% -> 23% of each run, Pallas kernels for 0% -> 10%
where the time goes in v1:
time: 241 us; the launch traced here: 240 us
  other arithmetic  77.4 us (32%)
  local copies, waits for them, and re-layouts  71.7 us (30%)
  Pallas kernels  62.1 us (26%)
  matrix products  16 us (7%)
  starting transfers between devices  11.1 us (5%)
    scatter-add x2, other arithmetic, operate(): return images.at[:, rows].add(received)  38.7 us
    pallas_call x2, Pallas kernels, summed_everywhere(): pl.pallas_call(functools.partial(doubling_kernel, bits), out_shape=jax.Sh...  38.3 us
    gather x2, local copies, waits for them, and re-layouts, operate(): values = jnp.take(vectors, rows, axis=1) * weights[None, :]  26.2 us
    pallas_call x2, Pallas kernels, block_product(): pl.pallas_call(stencil_kernel, out_shape=jax.ShapeDtypeStruct((columns, w...  23.9 us
    unnamed x31, local copies, waits for them, and re-layouts  13.8 us
    another operation x3, other arithmetic, shards(): chol = jnp.linalg.cholesky(gram_b, symmetrize_input=False)  11.6 us
    another operation x2, other arithmetic, shards(): basis = jax.scipy.linalg.solve_triangular(chol, search, lower=True)  9.85 us
    ppermute x2, starting transfers between devices, halos(): lax.ppermute(tail, axis, [(i, i + 1) for i in range(ends)])  8.17 us
  transfers between devices with their start and end apart: 6, of which 0 were waited for; matrix products, arithmetic and copies ran while one was open for 23% of the time, Pallas kernels for 10%

profile of v1, /device:TPU:0, one launch (start us, length us, event | category | flops | bytes accessed | tf_op | source)
XLA Modules:
  0.0 240.1 jit_solution(7739862224369527839)
XLA Ops:
  0.7 2.0 fusion.27
  3.4 4.9 %collective-permute-start = (bf16[80,1024]{1,0:T(8,128)(2,1)}, bf16[80,1024]{1,0:T(8,128)(2,1)S(1)}, u32[]{:S(2)}, u32[]{:S(2)}) collective-permute-start(bf16[80,1024]{1,0:T(8,128)(2,1)} %get-tuple-element.10), channel_id=1, source_target_pairs={{0,1},{1,2},{2,3},{3,4},{4,5},{5,6},{6,7},{7,8},{8,9},{9,10},{10,1... | collective-permute-start | bytes 491528 | tf_op jit(solution)/shard_map/ppermute | solution.py:27
  9.8 3.3 %copy.38 = f32[80,8192]{0,1:T(8,128)} copy(f32[80,8192]{1,0:T(8,128)S(1)} %pad_maximum_fusion.1.x_ref) | data formatting | bytes 5242880 | tf_op jit(solution)/shard_map/concatenate | solution.py:156
  13.8 13.1 %gather_fusion = f32[3072,80]{1,0:T(8,128)} fusion(f32[80,8192]{0,1:T(8,128)} %copy.38, s32[3072]{0:T(1024)S(1)} %broadcast_clamp_fusion), kind=kCustom, calls=%fused_computation | custom fusion | bytes 1978368 | tf_op jit(solution)/shard_map/jit(_take)/gather | solution.py:132
  26.9 3.6 %fusion.8 = bf16[80,3072]{0,1:T(8,128)(2,1)} fusion(f32[3072,80]{1,0:T(8,128)} %gather_fusion, f32[3072]{0:T(1024)S(1)} %fusion.20, pred[3072]{0:T(1024)(128)(4,1)S(1)} %compare_and_fusion), kind=kLoop, calls=%fused_computation.24 | loop fusion | flops 737280 | bytes 1489920 | tf_op jit(solution)/shard_map/convert_element_type | solution.py:14
  32.1 2.1 fusion
  34.7 2.8 %copy-done = bf16[1,3,4,512,512]{4,3,2,1,0:T(8,128)(2,1)S(1)} copy-done((bf16[1,3,4,512,512]{4,3,2,1,0:T(8,128)(2,1)S(1)}, bf16[1,3,4,512,512]{4,3,2,1,0:T(8,128)(2,1)}, u32[]{:S(2)}) %copy-start) | copy-done | bytes 6291480
  37.5 12.1 %shard_map.95 = f32[80,8192]{1,0:T(8,128)S(1)} custom-call(s32[3,18]{1,0:T(4,128)S(1)} %pad_dynamic-slice_fusion.1.kinds, f32[3,18]{1,0:T(4,128)S(1)} %pad_dynamic-slice_fusion.scales, f32[80,8192]{1,0:T(8,128)S(1)} %pad_maximum_fusion.1.x_ref, bf16[80,1024]{1,0:T(8,128)(2,1)S(1)} %collective-permute-done.before, ...), custom_call_target="tpu_custom_call" | custom-call | flops 3355443200 | bytes 10485760 | tf_op jit(solution)/shard_map/pallas_call | solution.py:117
  49.6 1.5 copy-done.2
  51.1 4.9 %copy.40 = f32[80,8192]{0,1:T(8,128)} copy(f32[80,8192]{1,0:T(8,128)} %copy-done.2) | data formatting | bytes 5242880 | tf_op jit(solution)/shard_map/pallas_call | solution.py:117
  57.5 19.4 %scatter_fusion = f32[80,8192]{0,1:T(8,128)} fusion(f32[80,8192]{0,1:T(8,128)} %copy.40, s32[3072]{0:T(1024)S(1)} %bitcast.93, f32[3072,80]{1,0:T(8,128)S(1)} %copy.41), kind=kCustom, calls=%fused_computation.2 | custom fusion | flops 245760 | bytes 2961408 | tf_op jit(solution)/shard_map/scatter-add | solution.py:135
  76.9 7.9 %fusion.29 = (f32[40,8192]{0,1:T(8,128)}, f32[40,8192]{0,1:T(8,128)}) fusion(f32[80,8192]{0,1:T(8,128)} %scatter_fusion), kind=kLoop, calls=%fused_computation.78 | loop fusion | bytes 5242880 | tf_op jit(solution)/shard_map/slice | solution.py:158
  84.8 2.9 %copy.59 = f32[40,8192]{1,0:T(8,128)S(1)} copy(f32[40,8192]{0,1:T(8,128)} %get-tuple-element.8) | data formatting | bytes 2621440
  88.8 18.3 %shard_map.96 = f32[8,128]{1,0:T(8,128)} custom-call(f32[8,128]{1,0:T(8,128)} %select_maximum_fusion.x_ref), custom_call_target="tpu_custom_call" | custom-call | tf_op jit(solution)/shard_map/pallas_call | solution.py:67
  107.9 3.6 %copy.60 = f32[40,8192]{1,0:T(8,128)} copy(f32[40,8192]{0,1:T(8,128)} %get-tuple-element.7) | data formatting | bytes 2621440
  111.5 1.6 fusion.28
  113.1 3.3 %collective-permute-start.3 = (bf16[40,1024]{1,0:T(8,128)(2,1)S(1)}, bf16[40,1024]{1,0:T(8,128)(2,1)S(1)}, u32[]{:S(2)}, u32[]{:S(2)}) collective-permute-start(bf16[40,1024]{1,0:T(8,128)(2,1)S(1)} %get-tuple-element.12), channel_id=1, source_target_pairs={{0,1},{1,2},{2,3},{3,4},{4,5},{5,6},{6,7},{7,8},{8,9},{9,10},{10,1... | collective-permute-start | bytes 245768 | tf_op jit(solution)/shard_map/ppermute | solution.py:27
  116.4 1.5 collective-permute-start.4
  117.9 2.7 %copy.44 = f32[40,8192]{0,1:T(8,128)} copy(f32[40,8192]{1,0:T(8,128)S(1)} %get-tuple-element.6.x_ref) | data formatting | bytes 2621440 | tf_op jit(solution)/shard_map/div | solution.py:174
  120.6 13.1 %gather_fusion.1 = f32[3072,40]{1,0:T(8,128)} fusion(f32[40,8192]{0,1:T(8,128)} %copy.44, s32[3072]{0:T(1024)S(1)} %broadcast_clamp_fusion), kind=kCustom, calls=%fused_computation.1 | custom fusion | bytes 995328 | tf_op jit(solution)/shard_map/jit(_take)/gather | solution.py:132
  133.7 3.5 %fusion.9 = bf16[40,3072]{0,1:T(8,128)(2,1)} fusion(f32[3072,40]{1,0:T(8,128)} %gather_fusion.1, f32[3072]{0:T(1024)S(1)} %fusion.20, pred[3072]{0:T(1024)(128)(4,1)S(1)} %compare_and_fusion), kind=kLoop, calls=%fused_computation.25 | loop fusion | flops 368640 | bytes 752640 | tf_op jit(solution)/shard_map/convert_element_type | solution.py:14
  138.7 3.6 %fusion.7 = f32[120,120]{0,1:T(8,128)S(1)} fusion(f32[40,8192]{1,0:T(8,128)} %bitcast.88, f32[40,8192]{1,0:T(8,128)S(1)} %get-tuple-element.6.x_ref, f32[40,8192]{1,0:T(8,128)S(1)} %bitcast.84), kind=kOutput, calls=%fused_computation.15 | convolution fusion | flops 709754880 | bytes 3989760 | tf_op jit(solution)/shard_map/dot_general | solution.py:179
  142.4 2.8 %copy-done.1 = bf16[1,3,4,512,512]{4,3,2,1,0:T(8,128)(2,1)S(1)} copy-done((bf16[1,3,4,512,512]{4,3,2,1,0:T(8,128)(2,1)S(1)}, bf16[1,3,4,512,512]{4,3,2,1,0:T(8,128)(2,1)}, u32[]{:S(2)}) %copy-start.1) | copy-done | bytes 6291480
  145.1 11.8 %shard_map.97 = f32[40,8192]{1,0:T(8,128)S(1)} custom-call(s32[3,18]{1,0:T(4,128)S(1)} %pad_dynamic-slice_fusion.1.kinds, f32[3,18]{1,0:T(4,128)S(1)} %pad_dynamic-slice_fusion.scales, f32[40,8192]{1,0:T(8,128)S(1)} %get-tuple-element.6.x_ref, bf16[40,1024]{1,0:T(8,128)(2,1)S(1)} %collective-permute-done.3.before, ...), custom_call_target="tpu_custom_call" | custom-call | flops 1677721600 | bytes 5242880 | tf_op jit(solution)/shard_map/pallas_call | solution.py:117
  156.9 2.7 %copy.46 = f32[40,8192]{0,1:T(8,128)} copy(f32[40,8192]{1,0:T(8,128)S(1)} %shard_map.97) | data formatting | bytes 2621440 | tf_op jit(solution)/shard_map/pallas_call | solution.py:117
  161.0 19.3 %scatter_fusion.1 = f32[40,8192]{0,1:T(8,128)} fusion(f32[40,8192]{0,1:T(8,128)} %copy.46, s32[3072]{0:T(1024)S(1)} %bitcast.94, f32[3072,40]{1,0:T(8,128)S(1)} %copy.47), kind=kCustom, calls=%fused_computation.3 | custom fusion | flops 122880 | bytes 1486848 | tf_op jit(solution)/shard_map/scatter-add | solution.py:135
  180.4 3.7 %copy.49 = f32[40,8192]{1,0:T(8,128)} copy(f32[40,8192]{0,1:T(8,128)} %scatter_fusion.1) | data formatting | bytes 2621440 | tf_op jit(solution)/shard_map/scatter-add | solution.py:135
  184.1 4.4 %fusion.1 = f32[120,120]{1,0:T(8,128)S(1)} fusion(f32[40,8192]{1,0:T(8,128)} %copy.60, f32[40,8192]{1,0:T(8,128)} %copy.49, f32[40,8192]{1,0:T(8,128)} %copy-done.6, f32[40,8192]{1,0:T(8,128)} %bitcast.89, f32[40,8192]{1,0:T(8,128)S(1)} %get-tuple-element.6.x_ref, f32[40,8192]{1,0:T(8,128)S(1)} %bitcast.85), kind=kOutput, calls=%fused_computation.8 | convolution fusion | flops 711720960 | bytes 7921920 | tf_op jit(solution)/shard_map/dot_general | solution.py:180
  189.3 19.9 %shard_map.98 = f32[120,128]{1,0:T(8,128)} custom-call(f32[120,128]{1,0:T(8,128)} %copy.51.x_ref), custom_call_target="tpu_custom_call" | custom-call | tf_op jit(solution)/shard_map/pallas_call | solution.py:67
  210.5 11.0 %cholesky.16 = f32[120,120]{1,0:T(8,128)S(1)} custom-call(f32[120,120]{1,0:T(8,128)S(1)} %fusion.17), custom_call_target="Cholesky" | custom-call | tf_op jit(solution)/shard_map/jit(cholesky)/cholesky | solution.py:196
  222.8 9.2 %custom-call.10 = f32[1,120,120]{1,2,0:T(8,128)S(1)} custom-call(f32[1,120,120]{2,1,0:T(8,128)S(1)} %fusion.10), custom_call_target="InvertDiagBlocksLowerTriangular" | custom-call | tf_op jit(solution)/shard_map/jit(_solve_triangular)/triangular_solve | solution.py:199
  232.0 6.7 %convolution_bitcast_fusion = f32[1,120,8192]{2,1,0:T(8,128)} fusion(f32[40,8192]{1,0:T(8,128)} %bitcast.90, f32[40,8192]{1,0:T(8,128)S(1)} %get-tuple-element.6.x_ref, f32[40,8192]{1,0:T(8,128)S(1)} %bitcast.86, f32[1,120,120]{1,2,0:T(8,128)S(1)} %custom-call.10), kind=kOutput, calls=%fused_computation.4 | convolution fusion | flops 1417543680 | bytes 7921920 | tf_op jit(solution)/shard_map/jit(_solve_triangular)/triangular_solve | solution.py:199
  (72 shorter events, 15.2 us)
Async XLA Ops:
  0.6 9.0 %copy-start.3 = (f32[1,40,8192]{2,1,0:T(8,128)S(1)}, f32[1,40,8192]{2,1,0:T(8,128)}, u32[]{:S(2)}) copy-start(f32[1,40,8192]{2,1,0:T(8,128)} %param.10) | copy-start | bytes 3932164
  0.6 9.0 %copy-start.7 = (f32[1,40,8192]{2,1,0:T(8,128)S(1)}, f32[1,40,8192]{2,1,0:T(8,128)}, u32[]{:S(2)}) copy-start(f32[1,40,8192]{2,1,0:T(8,128)} %param.11) | copy-start | bytes 3932164
  3.4 31.3 %collective-permute-start = (bf16[80,1024]{1,0:T(8,128)(2,1)}, bf16[80,1024]{1,0:T(8,128)(2,1)S(1)}, u32[]{:S(2)}, u32[]{:S(2)}) collective-permute-start(bf16[80,1024]{1,0:T(8,128)(2,1)} %get-tuple-element.10), channel_id=1, source_target_pairs={{0,1},{1,2},{2,3},{3,4},{4,5},{5,6},{6,7},{7,8},{8,9},{9,10},{10,1... | collective-permute-start | bytes 491528 | tf_op jit(solution)/shard_map/ppermute | solution.py:27
  8.3 1.5 copy-start.8
  8.3 26.4 %collective-permute-start.1 = (bf16[80,1024]{1,0:T(8,128)(2,1)}, bf16[80,1024]{1,0:T(8,128)(2,1)S(1)}, u32[]{:S(2)}, u32[]{:S(2)}) collective-permute-start(bf16[80,1024]{1,0:T(8,128)(2,1)} %get-tuple-element.9), channel_id=1, source_target_pairs={{1,0},{2,1},{3,2},{4,3},{5,4},{6,5},{7,6},{8,7},{9,8},{10,9},{11,1... | collective-permute-start | bytes 491528 | tf_op jit(solution)/shard_map/ppermute | solution.py:28
  13.8 13.1 %copy-start.9 = (f32[3072]{0:T(1024)S(1)}, f32[3072]{0:T(1024)}, u32[]{:S(2)}) copy-start(f32[3072]{0:T(1024)} %param.17) | copy-start | bytes 36868
  31.9 2.3 copy-start.10
  31.9 2.5 %copy-start.11 = (s32[1,3,256]{2,0,1:T(1,128)S(1)}, s32[1,3,256]{2,0,1:T(1,128)}, u32[]{:S(2)}) copy-start(s32[1,3,256]{2,0,1:T(1,128)} %param.12) | copy-start | bytes 9220
  31.9 24.0 %collective-permute-start.2 = (bf16[80,3072]{1,0:T(8,128)(2,1)S(1)}, bf16[80,3072]{1,0:T(8,128)(2,1)}, u32[]{:S(2)}, u32[]{:S(2)}) collective-permute-start(bf16[80,3072]{1,0:T(8,128)(2,1)S(1)} %copy.39), channel_id=1, source_target_pairs={{0,16},{16,0},{1,17},{17,1},{2,18},{18,2},{3,19},{19,3},{4,20},{20... | collective-permute-start | bytes 1474568 | tf_op jit(solution)/shard_map/ppermute | solution.py:18
  34.7 2.8 %copy-start = (bf16[1,3,4,512,512]{4,3,2,1,0:T(8,128)(2,1)S(1)}, bf16[1,3,4,512,512]{4,3,2,1,0:T(8,128)(2,1)}, u32[]{:S(2)}) copy-start(bf16[1,3,4,512,512]{4,3,2,1,0:T(8,128)(2,1)} %param.14) | copy-start | bytes 18874372
  49.6 1.5 copy-start.2
  84.8 2.9 %copy-start.4 = (f32[1,40,8192]{2,1,0:T(8,128)S(1)}, f32[1,40,8192]{2,1,0:T(8,128)}, u32[]{:S(2)}) copy-start(f32[1,40,8192]{2,1,0:T(8,128)} %param.10) | copy-start | bytes 3932164
  87.7 23.8 %copy-start.6 = (f32[40,8192]{1,0:T(8,128)}, f32[40,8192]{1,0:T(8,128)S(1)}, u32[]{:S(2)}) copy-start(f32[40,8192]{1,0:T(8,128)S(1)} %copy.59) | copy-start | bytes 3932164
  113.1 29.2 %collective-permute-start.3 = (bf16[40,1024]{1,0:T(8,128)(2,1)S(1)}, bf16[40,1024]{1,0:T(8,128)(2,1)S(1)}, u32[]{:S(2)}, u32[]{:S(2)}) collective-permute-start(bf16[40,1024]{1,0:T(8,128)(2,1)S(1)} %get-tuple-element.12), channel_id=1, source_target_pairs={{0,1},{1,2},{2,3},{3,4},{4,5},{5,6},{6,7},{7,8},{8,9},{9,10},{10,1... | collective-permute-start | bytes 245768 | tf_op jit(solution)/shard_map/ppermute | solution.py:27
  116.4 25.9 %collective-permute-start.4 = (bf16[40,1024]{1,0:T(8,128)(2,1)S(1)}, bf16[40,1024]{1,0:T(8,128)(2,1)S(1)}, u32[]{:S(2)}, u32[]{:S(2)}) collective-permute-start(bf16[40,1024]{1,0:T(8,128)(2,1)S(1)} %get-tuple-element.11), channel_id=1, source_target_pairs={{1,0},{2,1},{3,2},{4,3},{5,4},{6,5},{7,6},{8,7},{9,8},{10,9},{11,1... | collective-permute-start | bytes 245768 | tf_op jit(solution)/shard_map/ppermute | solution.py:28
  138.6 21.0 %collective-permute-start.5 = (bf16[40,3072]{1,0:T(8,128)(2,1)S(1)}, bf16[40,3072]{1,0:T(8,128)(2,1)}, u32[]{:S(2)}, u32[]{:S(2)}) collective-permute-start(bf16[40,3072]{1,0:T(8,128)(2,1)S(1)} %copy.45), channel_id=1, source_target_pairs={{0,16},{16,0},{1,17},{17,1},{2,18},{18,2},{3,19},{19,3},{4,20},{20... | collective-permute-start | bytes 737288 | tf_op jit(solution)/shard_map/ppermute | solution.py:18
  142.3 2.8 %copy-start.1 = (bf16[1,3,4,512,512]{4,3,2,1,0:T(8,128)(2,1)S(1)}, bf16[1,3,4,512,512]{4,3,2,1,0:T(8,128)(2,1)}, u32[]{:S(2)}) copy-start(bf16[1,3,4,512,512]{4,3,2,1,0:T(8,128)(2,1)} %param.14) | copy-start | bytes 18874372
  180.4 3.7 %copy-start.5 = (f32[1,40,8192]{2,1,0:T(8,128)S(1)}, f32[1,40,8192]{2,1,0:T(8,128)}, u32[]{:S(2)}) copy-start(f32[1,40,8192]{2,1,0:T(8,128)} %param.10) | copy-start | bytes 3932164

commit v2 on v1

--- a/solution.py
+++ b/solution.py
@@ -8,10 +8,8 @@
 from jax.sharding import PartitionSpec as P
 
 BS = 512
-
-
-def for_sending(shard):
-    return jax.tree.map(lambda a: a.astype(jnp.bfloat16) if a.dtype == jnp.float32 else a, shard)
+LANES = 128
+SHIFT = 16
 
 
 def swapped(shard, axis, apart):
@@ -85,12 +83,25 @@
 NT = (((1,), (1,)), ((), ()))
 
 
-def stencil_kernel(kinds, scales, x_ref, before, after, tables, o_ref, window):
-    nbr = x_ref.shape[1] // BS
-    wide = x_ref.shape[1]
+def operator_kernel(
+    kinds, scales, places, weights, x_ref, before, after, other, tables, o_ref, window, rows_in, rows_out
+):
+    columns, wide = x_ref.shape
+    nbr = wide // BS
+    share = places.shape[0] // nbr
     window[:, : 2 * BS] = before[...]
     window[:, 2 * BS : 2 * BS + wide] = x_ref[...].astype(jnp.bfloat16)
     window[:, 2 * BS + wide :] = after[...]
+    blank = jnp.zeros((LANES - columns, LANES), jnp.float32)
+
+    def turn_in(tile, carry):
+        span = pl.ds(pl.multiple_of(tile * LANES, LANES), LANES)
+        cell = jnp.concatenate([other[:, span].astype(jnp.float32), blank], axis=0)
+        rows_in[span, :] = cell.T
+        rows_out[span, :] = jnp.zeros((LANES, LANES), jnp.float32)
+        return carry
+
+    lax.fori_loop(0, wide // LANES, turn_in, 0, unroll=2)
 
     def term(n, shift, offset, at, dims):
         block = window[:, pl.ds(pl.multiple_of((n + 2 + shift) * BS, BS), BS)]
@@ -105,34 +116,45 @@
             total = total + term(n, offset, offset, n + 2, NT)
             total = total + term(n, -offset, offset, n + 2 - offset, NN)
         o_ref[:, pl.ds(pl.multiple_of(n * BS, BS), BS)] = total
+        for slot in range(share):
+            place = places[n * share + slot]
+            source = lax.shift_right_logical(place, SHIFT)
+            target = lax.bitwise_and(place, (1 << SHIFT) - 1)
+            rows_out[pl.ds(target, 1), :] = rows_in[pl.ds(source, 1), :] * weights[n * share + slot]
         return carry
 
     lax.fori_loop(0, nbr, step, 0)
 
-
-def block_product(vectors, sides, kinds, scales, tables):
+    def turn_out(tile, carry):
+        span = pl.ds(pl.multiple_of(tile * LANES, LANES), LANES)
+        o_ref[:, span] = o_ref[:, span] + rows_out[span, :].T[:columns]
+        return carry
+
+    lax.fori_loop(0, wide // LANES, turn_out, 0, unroll=2)
+
+
+def operate(vectors, kinds, scales, tables, places, weights):
     columns, wide = vectors.shape
+    rounded = vectors.astype(jnp.bfloat16)
+    other = swapped(rounded, "field", 0)
+    before, after = halos(rounded, "dom", 1, 2 * BS)
     smem = pl.BlockSpec(memory_space=pltpu.SMEM)
     vmem = pl.BlockSpec(memory_space=pltpu.VMEM)
     return pl.pallas_call(
-        stencil_kernel,
+        operator_kernel,
         out_shape=jax.ShapeDtypeStruct((columns, wide), jnp.float32),
-        in_specs=[smem, smem, vmem, vmem, vmem, vmem],
+        in_specs=[smem, smem, smem, smem, vmem, vmem, vmem, vmem, vmem],
         out_specs=vmem,
-        scratch_shapes=[pltpu.VMEM((columns, wide + 4 * BS), jnp.bfloat16)],
+        scratch_shapes=[
+            pltpu.VMEM((columns, wide + 4 * BS), jnp.bfloat16),
+            pltpu.VMEM((wide, LANES), jnp.float32),
+            pltpu.VMEM((wide, LANES), jnp.float32),
+        ],
         cost_estimate=pl.CostEstimate(
             flops=10 * columns * wide * BS, bytes_accessed=16 * columns * wide, transcendentals=0
         ),
-        compiler_params=pltpu.CompilerParams(vmem_limit_bytes=30 * 1024 * 1024),
-    )(kinds, scales, vectors, *sides, tables)
-
-
-def operate(vectors, kinds, scales, tables, rows, weights):
-    sides = halos(vectors.astype(jnp.bfloat16), "dom", 1, 2 * BS)
-    values = jnp.take(vectors, rows, axis=1) * weights[None, :]
-    received = swapped(for_sending(values), "field", 0).astype(values.dtype)
-    images = block_product(vectors, sides, kinds, scales, tables)
-    return images.at[:, rows].add(received)
+        compiler_params=pltpu.CompilerParams(vmem_limit_bytes=40 * 1024 * 1024),
+    )(kinds, scales, places, weights, vectors, before, after, other, tables)
 
 
 def shards(modes, previous, kinds, scales, tables, wet_rows, wet_counts, coupling):
@@ -152,7 +174,8 @@
     slots = coupling.shape[0]
     used = jnp.arange(slots, dtype=jnp.int32) < wet_counts[0]
     weights = jnp.where(used, coupling, jnp.float32(0.0))
-    operands = (local_kinds, local_scales, field_tables, rows, weights)
+    places = (swapped(rows, "field", 0) << SHIFT) | rows
+    operands = (local_kinds, local_scales, field_tables, places, weights)
     first_pair = jnp.concatenate([vec_modes, vec_prev], axis=0)
     image_pair = operate(first_pair, *operands)
     image_x, image_p = image_pair[:columns], image_pair[columns:]

time: 241 us -> 155 us (0.64)
  local copies, waits for them, and re-layouts: 71.7 us -> 4.81 us
  other arithmetic: 77.4 us -> 34.7 us
  Pallas kernels: 62.1 us -> 85.4 us
  waiting for transfers between devices: 0.02 us -> 2.71 us
    scatter-add x2 -> x0, other arithmetic: 38.7 us -> none  [operate(): return images.at[:, rows].add(received)]
    gather x2 -> x0, local copies, waits for them, and re-layouts: 26.2 us -> none  [operate(): values = jnp.take(vectors, rows, axis=1) * weights[None, :]]
    pallas_call x2, Pallas kernels: 23.9 us -> 47.5 us  [operate(): pl.pallas_call(operator_kernel, out_shape=jax.ShapeDtypeStruct((columns,...]
    unnamed x31 -> x35, local copies, waits for them, and re-layouts: 13.8 us -> 0.93 us
    slice x1 -> x0, local copies, waits for them, and re-layouts: 7.9 us -> none  [shards(): image_x, image_p = (image_pair[:columns], image_pair[columns:])]
    convert_element_type x6 -> x2, other arithmetic: 12.8 us -> 5.18 us  [operate(): rounded = vectors.astype(jnp.bfloat16)]
    pallas_call x2 -> x0, local copies, waits for them, and re-layouts: 7.54 us -> none  [block_product(): pl.pallas_call(stencil_kernel, out_shape=jax.ShapeDtypeStruct((columns, w...]
    scatter-add x1 -> x0, local copies, waits for them, and re-layouts: 3.74 us -> none  [operate(): return images.at[:, rows].add(received)]
  transfers between devices with their start and end apart: 6 -> 7, of which waited for: 0 -> 2; matrix products, arithmetic and copies ran while one was open for 23% -> 7% of each run, Pallas kernels for 10% -> 0%
where the time goes in v2:
time: 155 us; the launch traced here: 154 us
  Pallas kernels  85.4 us (55%)
  other arithmetic  34.7 us (22%)
  matrix products  13.9 us (9%)
  starting transfers between devices  10.9 us (7%)
  local copies, waits for them, and re-layouts  4.81 us (3%)
  waiting for transfers between devices  2.71 us (2%)
  between operations  1.84 us (1%)
    pallas_call x2, Pallas kernels, operate(): pl.pallas_call(operator_kernel, out_shape=jax.ShapeDtypeStruct((columns,...  47.5 us
    pallas_call x2, Pallas kernels, summed_everywhere(): pl.pallas_call(functools.partial(doubling_kernel, bits), out_shape=jax.Sh...  37.9 us
    another operation x3, other arithmetic, shards(): chol = jnp.linalg.cholesky(gram_b, symmetrize_input=False)  11.6 us
    another operation x2, other arithmetic, shards(): basis = jax.scipy.linalg.solve_triangular(chol, search, lower=True)  9.85 us
    ppermute x2, starting transfers between devices, halos(): lax.ppermute(tail, axis, [(i, i + 1) for i in range(ends)])  7.44 us
    another operation x1, matrix products, shards(): basis = jax.scipy.linalg.solve_triangular(chol, search, lower=True)  6.71 us
    convert_element_type x2, other arithmetic, operate(): rounded = vectors.astype(jnp.bfloat16)  5.18 us
    dot_general x1, matrix products, shards(): part_b = jnp.dot(search, search.T, precision=high)  4.2 us
  transfers between devices with their start and end apart: 7, of which 2 were waited for; matrix products, arithmetic and copies ran while one was open for 7% of the time, Pallas kernels for 0%

profile of v2, /device:TPU:0, one launch (start us, length us, event | category | flops | bytes accessed | tf_op | source)
XLA Modules:
  0.0 154.2 jit_solution(470452256980364005)
XLA Ops:
  0.7 3.1 %fusion.25 = bf16[80,8192]{1,0:T(8,128)(2,1)} fusion(f32[40,8192]{1,0:T(8,128)} %bitcast.80, f32[40,8192]{1,0:T(8,128)} %bitcast.75), kind=kLoop, calls=%fused_computation.63 | loop fusion | flops 2621440 | bytes 3932160 | tf_op jit(solution)/shard_map/convert_element_type | solution.py:138
  3.7 0.5 collective-permute-start.3
  4.2 1.7 %fusion.27 = (bf16[80,1024]{1,0:T(8,128)(2,1)}, bf16[80,1024]{1,0:T(8,128)(2,1)}) fusion(bf16[80,8192]{1,0:T(8,128)(2,1)} %fusion.25), kind=kLoop, calls=%fused_computation.65 | loop fusion | bytes 655360 | tf_op jit(solution)/shard_map/slice | solution.py:22
  6.0 5.0 %collective-permute-start.1 = (bf16[80,1024]{1,0:T(8,128)(2,1)}, bf16[80,1024]{1,0:T(8,128)(2,1)}, u32[]{:S(2)}, u32[]{:S(2)}) collective-permute-start(bf16[80,1024]{1,0:T(8,128)(2,1)} %get-tuple-element.10), channel_id=1, source_target_pairs={{0,1},{1,2},{2,3},{3,4},{4,5},{5,6},{6,7},{7,8},{8,9},{9,10},{10,1... | collective-permute-start | bytes 491528 | tf_op jit(solution)/shard_map/ppermute | solution.py:25
  11.0 1.3 collective-permute-start.2
  12.6 0.8 iota_compare_fusion
  14.5 2.2 %fusion = f32[4,512]{1,0:T(4,128)S(1)} fusion(bf16[1,3,4,512,512]{4,3,2,1,0:T(8,128)(2,1)} %param.14, pred[512,512]{1,0:T(8,128)(4,1)} %iota_compare_fusion), kind=kLoop, calls=%fused_computation.2 | loop fusion | flops 3143680 | bytes 2367488 | tf_op jit(solution)/shard_map/reduce_sum | solution.py:188
  16.8 1.5 pad_maximum_fusion.1.x_ref
  18.4 1.8 %collective-permute-done.2.after = bf16[80,1024]{1,0:T(8,128)(2,1)} collective-permute-done((bf16[80,1024]{1,0:T(8,128)(2,1)}, bf16[80,1024]{1,0:T(8,128)(2,1)}, u32[]{:S(2)}, u32[]{:S(2)}) %collective-permute-start.2) | collective-permute-done | bytes 163872 | tf_op jit(solution)/shard_map/ppermute | solution.py:26
  20.3 24.0 %shard_map.95 = f32[80,8192]{1,0:T(8,128)S(1)} custom-call(s32[3,18]{1,0:T(4,128)S(1)} %pad_dynamic-slice_fusion.1.kinds, f32[3,18]{1,0:T(4,128)S(1)} %pad_dynamic-slice_fusion.scales, s32[3072]{0:T(1024)S(1)} %shift-left_or_fusion.places, f32[3072]{0:T(1024)S(1)} %fusion.18.weights, f32[80,8192]{1,0:T(8,128)S(1)} %pad_maximum_fusion.1.x_ref, ...), custom_call_target="tpu_custom_call" | custom-call | flops 3355443200 | bytes 10485760 | tf_op jit(solution)/shard_map/pallas_call | solution.py:143
  44.3 1.8 %multiply_reduce_fusion.1 = (f32[40]{0:T(128)S(1)}, f32[40]{0:T(128)S(1)}, f32[40,8192]{1,0:T(8,128)}, f32[40,8192]{1,0:T(8,128)}) fusion(f32[1,40,8192]{2,1,0:T(8,128)S(1)} %copy-done.1, f32[80,8192]{1,0:T(8,128)S(1)} %shard_map.95), kind=kLoop, calls=%fused_computation.14 | loop fusion | flops 1310640 | bytes 6553920 | tf_op jit(solution)/shard_map/reduce_sum | solution.py:183
  46.2 0.7 copy-done
  46.8 0.6 select_maximum_fusion.x_ref
  47.4 16.6 %shard_map.96 = f32[8,128]{1,0:T(8,128)} custom-call(f32[8,128]{1,0:T(8,128)} %select_maximum_fusion.x_ref), custom_call_target="tpu_custom_call" | custom-call | tf_op jit(solution)/shard_map/pallas_call | solution.py:65
  64.0 0.8 fusion.19
  64.8 2.1 %fusion.26 = (bf16[40,8192]{1,0:T(8,128)(2,1)S(1)}, f32[40,8192]{1,0:T(8,128)S(1)}) fusion(f32[8192]{0:T(1024)S(1)} %bitcast.85, f32[40]{0:T(128)S(1)} %fusion.19, f32[1,40,8192]{2,1,0:T(8,128)} %param.10, f32[80,8192]{1,0:T(8,128)} %copy-done), kind=kLoop, calls=%fused_computation.64 | loop fusion | flops 1310720 | bytes 4620448 | tf_op jit(solution)/shard_map/convert_element_type | solution.py:138
  67.0 2.4 %collective-permute-start.4 = (bf16[40,1024]{1,0:T(8,128)(2,1)S(1)}, bf16[40,1024]{1,0:T(8,128)(2,1)S(1)}, u32[]{:S(2)}, u32[]{:S(2)}) collective-permute-start(bf16[40,1024]{1,0:T(8,128)(2,1)S(1)} %get-tuple-element.12), channel_id=1, source_target_pairs={{0,1},{1,2},{2,3},{3,4},{4,5},{5,6},{6,7},{7,8},{8,9},{9,10},{10,1... | collective-permute-start | bytes 245768 | tf_op jit(solution)/shard_map/ppermute | solution.py:25
  69.4 1.3 collective-permute-start.5
  70.7 4.2 %fusion.7 = f32[120,120]{0,1:T(8,128)S(1)} fusion(f32[40,8192]{1,0:T(8,128)} %bitcast.82, f32[40,8192]{1,0:T(8,128)S(1)} %get-tuple-element.6.x_ref, f32[40,8192]{1,0:T(8,128)} %bitcast.76), kind=kOutput, calls=%fused_computation.11 | convolution fusion | flops 709754880 | bytes 3989760 | tf_op jit(solution)/shard_map/dot_general | solution.py:202
  75.0 0.9 collective-permute-done.5.after
  75.9 23.5 %shard_map.97 = f32[40,8192]{1,0:T(8,128)S(1)} custom-call(s32[3,18]{1,0:T(4,128)S(1)} %pad_dynamic-slice_fusion.1.kinds, f32[3,18]{1,0:T(4,128)S(1)} %pad_dynamic-slice_fusion.scales, s32[3072]{0:T(1024)S(1)} %shift-left_or_fusion.places, f32[3072]{0:T(1024)S(1)} %fusion.18.weights, f32[40,8192]{1,0:T(8,128)S(1)} %get-tuple-element.6.x_ref, ...), custom_call_target="tpu_custom_call" | custom-call | flops 1677721600 | bytes 5242880 | tf_op jit(solution)/shard_map/pallas_call | solution.py:143
  99.4 1.8 %fusion.1 = f32[120,120]{1,0:T(8,128)S(1)} fusion(f32[40,8192]{1,0:T(8,128)S(1)} %copy-done.6, f32[40,8192]{1,0:T(8,128)S(1)} %shard_map.97, f32[40,8192]{1,0:T(8,128)S(1)} %copy-done.5, f32[40,8192]{1,0:T(8,128)S(1)} %bitcast.84, f32[40,8192]{1,0:T(8,128)S(1)} %get-tuple-element.6.x_ref, f32[40,8192]{1,0:T(8,128)S(1)} %bitcast.78), kind=kOutput, calls=%fused_computation.4 | convolution fusion | flops 711720960 | bytes 7921920 | tf_op jit(solution)/shard_map/dot_general | solution.py:203
  101.4 0.7 copy.12.x_ref
  102.1 21.3 %shard_map.98 = f32[120,128]{1,0:T(8,128)} custom-call(f32[120,128]{1,0:T(8,128)} %copy.12.x_ref), custom_call_target="tpu_custom_call" | custom-call | tf_op jit(solution)/shard_map/pallas_call | solution.py:65
  123.4 1.0 fusion.29
  124.6 11.0 %cholesky.16 = f32[120,120]{1,0:T(8,128)S(1)} custom-call(f32[120,120]{1,0:T(8,128)S(1)} %fusion.15), custom_call_target="Cholesky" | custom-call | tf_op jit(solution)/shard_map/jit(cholesky)/cholesky | solution.py:219
  135.7 0.6 compare_reduce_fusion
  136.3 0.7 fusion.8
  137.0 9.2 %custom-call.10 = f32[1,120,120]{1,2,0:T(8,128)S(1)} custom-call(f32[1,120,120]{2,1,0:T(8,128)S(1)} %fusion.8), custom_call_target="InvertDiagBlocksLowerTriangular" | custom-call | tf_op jit(solution)/shard_map/jit(_solve_triangular)/triangular_solve | solution.py:222
  146.3 6.7 %convolution_bitcast_fusion = f32[1,120,8192]{2,1,0:T(8,128)} fusion(f32[40,8192]{1,0:T(8,128)} %bitcast.83, f32[40,8192]{1,0:T(8,128)S(1)} %get-tuple-element.6.x_ref, f32[40,8192]{1,0:T(8,128)S(1)} %bitcast.79, f32[1,120,120]{1,2,0:T(8,128)S(1)} %custom-call.10), kind=kOutput, calls=%fused_computation | convolution fusion | flops 1417543680 | bytes 7921920 | tf_op jit(solution)/shard_map/jit(_solve_triangular)/triangular_solve | solution.py:222
  153.0 0.3 convolution_bitcast_fusion.1
  153.3 0.9 fusion.12
  (60 shorter events, 1.4 us)
Async XLA Ops:
  0.6 11.7 %copy-start.8 = (s32[1,3072]{1,0:T(1,128)S(1)}, s32[1,3072]{1,0:T(1,128)}, u32[]{:S(2)}) copy-start(s32[1,3072]{1,0:T(1,128)} %param.15) | copy-start | bytes 36868
  0.6 12.8 %copy-start.9 = (f32[1,3,256]{2,0,1:T(1,128)S(1)}, f32[1,3,256]{2,0,1:T(1,128)}, u32[]{:S(2)}) copy-start(f32[1,3,256]{2,0,1:T(1,128)} %param.13) | copy-start | bytes 9220
  0.7 12.8 %copy-start.10 = (s32[1,3,256]{2,0,1:T(1,128)S(1)}, s32[1,3,256]{2,0,1:T(1,128)}, u32[]{:S(2)}) copy-start(s32[1,3,256]{2,0,1:T(1,128)} %param.12) | copy-start | bytes 9220
  0.7 19.6 %slice-start = ((s8[6291456]{0:T(1024)(128)(4,1)}), s8[2097152]{0:T(1024)(128)(4,1)S(1)}, s32[]{:S(2)}) async-start(s8[6291456]{0:T(1024)(128)(4,1)} %bitcast.69), calls=%async_computation | async-start | bytes 4194304
  3.7 16.5 %collective-permute-start.3 = (bf16[80,8192]{1,0:T(8,128)(2,1)}, bf16[80,8192]{1,0:T(8,128)(2,1)S(1)}, u32[]{:S(2)}, u32[]{:S(2)}) collective-permute-start(bf16[80,8192]{1,0:T(8,128)(2,1)} %fusion.25), channel_id=1, source_target_pairs={{0,16},{16,0},{1,17},{17,1},{2,18},{18,2},{3,19},{19,3},{4,20},{20... | collective-permute-start | bytes 3932168 | tf_op jit(solution)/shard_map/ppermute | solution.py:16
  6.0 12.5 %collective-permute-start.1 = (bf16[80,1024]{1,0:T(8,128)(2,1)}, bf16[80,1024]{1,0:T(8,128)(2,1)}, u32[]{:S(2)}, u32[]{:S(2)}) collective-permute-start(bf16[80,1024]{1,0:T(8,128)(2,1)} %get-tuple-element.10), channel_id=1, source_target_pairs={{0,1},{1,2},{2,3},{3,4},{4,5},{5,6},{6,7},{7,8},{8,9},{9,10},{10,1... | collective-permute-start | bytes 491528 | tf_op jit(solution)/shard_map/ppermute | solution.py:25
  11.0 9.2 %collective-permute-start.2 = (bf16[80,1024]{1,0:T(8,128)(2,1)}, bf16[80,1024]{1,0:T(8,128)(2,1)}, u32[]{:S(2)}, u32[]{:S(2)}) collective-permute-start(bf16[80,1024]{1,0:T(8,128)(2,1)} %get-tuple-element.9), channel_id=1, source_target_pairs={{1,0},{2,1},{3,2},{4,3},{5,4},{6,5},{7,6},{8,7},{9,8},{10,9},{11,1... | collective-permute-start | bytes 491528 | tf_op jit(solution)/shard_map/ppermute | solution.py:26
  12.3 6.1 %collective-permute-start = (s32[3072]{0:T(1024)S(1)}, s32[3072]{0:T(1024)S(1)}, u32[]{:S(2)}, u32[]{:S(2)}) collective-permute-start(s32[3072]{0:T(1024)S(1)} %bitcast.88), channel_id=1, source_target_pairs={{0,16},{16,0},{1,17},{17,1},{2,18},{18,2},{3,19},{19,3},{4,20},{20... | collective-permute-start | bytes 36872 | tf_op jit(solution)/shard_map/ppermute | solution.py:16
  13.4 3.4 %copy-start.1 = (f32[1,40,8192]{2,1,0:T(8,128)S(1)}, f32[1,40,8192]{2,1,0:T(8,128)}, u32[]{:S(2)}) copy-start(f32[1,40,8192]{2,1,0:T(8,128)} %param.10) | copy-start | bytes 3932164
  14.5 5.8 %slice-start.1 = ((s8[6291456]{0:T(1024)(128)(4,1)}), s8[4194304]{0:T(1024)(128)(4,1)S(1)}, s32[]{:S(2)}) async-start(s8[6291456]{0:T(1024)(128)(4,1)} %bitcast.69), calls=%async_computation.1 | async-start | bytes 8388608
  16.8 1.5 copy-start.7
  44.3 2.5 %copy-start = (f32[80,8192]{1,0:T(8,128)}, f32[80,8192]{1,0:T(8,128)S(1)}, u32[]{:S(2)}) copy-start(f32[80,8192]{1,0:T(8,128)S(1)} %shard_map.95) | copy-start | bytes 7864324
  44.3 31.6 %slice-start.2 = ((s8[6291456]{0:T(1024)(128)(4,1)}), s8[2097152]{0:T(1024)(128)(4,1)S(1)}, s32[]{:S(2)}) async-start(s8[6291456]{0:T(1024)(128)(4,1)} %bitcast.72), calls=%async_computation.2 | async-start | bytes 4194304
  64.8 11.1 %slice-start.3 = ((s8[6291456]{0:T(1024)(128)(4,1)}), s8[4194304]{0:T(1024)(128)(4,1)S(1)}, s32[]{:S(2)}) async-start(s8[6291456]{0:T(1024)(128)(4,1)} %bitcast.72), calls=%async_computation.3 | async-start | bytes 8388608
  66.9 9.0 %collective-permute-start.6 = (bf16[40,8192]{1,0:T(8,128)(2,1)S(1)}, bf16[40,8192]{1,0:T(8,128)(2,1)S(1)}, u32[]{:S(2)}, u32[]{:S(2)}) collective-permute-start(bf16[40,8192]{1,0:T(8,128)(2,1)S(1)} %get-tuple-element.5), channel_id=1, source_target_pairs={{0,16},{16,0},{1,17},{17,1},{2,18},{18,2},{3,19},{19,3},{4,20},{20... | collective-permute-start | bytes 1966088 | tf_op jit(solution)/shard_map/ppermute | solution.py:16
  67.0 8.0 %collective-permute-start.4 = (bf16[40,1024]{1,0:T(8,128)(2,1)S(1)}, bf16[40,1024]{1,0:T(8,128)(2,1)S(1)}, u32[]{:S(2)}, u32[]{:S(2)}) collective-permute-start(bf16[40,1024]{1,0:T(8,128)(2,1)S(1)} %get-tuple-element.12), channel_id=1, source_target_pairs={{0,1},{1,2},{2,3},{3,4},{4,5},{5,6},{6,7},{7,8},{8,9},{9,10},{10,1... | collective-permute-start | bytes 245768 | tf_op jit(solution)/shard_map/ppermute | solution.py:25
  69.4 6.5 %collective-permute-start.5 = (bf16[40,1024]{1,0:T(8,128)(2,1)S(1)}, bf16[40,1024]{1,0:T(8,128)(2,1)S(1)}, u32[]{:S(2)}, u32[]{:S(2)}) collective-permute-start(bf16[40,1024]{1,0:T(8,128)(2,1)S(1)} %get-tuple-element.11), channel_id=1, source_target_pairs={{1,0},{2,1},{3,2},{4,3},{5,4},{6,5},{7,6},{8,7},{9,8},{10,9},{11,1... | collective-permute-start | bytes 245768 | tf_op jit(solution)/shard_map/ppermute | solution.py:26
  74.9 24.5 %copy-start.2 = (f32[1,40,8192]{2,1,0:T(8,128)S(1)}, f32[1,40,8192]{2,1,0:T(8,128)}, u32[]{:S(2)}) copy-start(f32[1,40,8192]{2,1,0:T(8,128)} %param.10) | copy-start | bytes 3932164
  75.0 24.5 %copy-start.4 = (f32[1,40,8192]{2,1,0:T(8,128)S(1)}, f32[1,40,8192]{2,1,0:T(8,128)}, u32[]{:S(2)}) copy-start(f32[1,40,8192]{2,1,0:T(8,128)} %param.11) | copy-start | bytes 3932164
  75.0 24.5 %copy-start.5 = (f32[40,8192]{1,0:T(8,128)S(1)}, f32[40,8192]{1,0:T(8,128)}, u32[]{:S(2)}) copy-start(f32[40,8192]{1,0:T(8,128)} %get-tuple-element.7) | copy-start | bytes 3932164
  75.0 24.5 %copy-start.6 = (f32[40,8192]{1,0:T(8,128)S(1)}, f32[40,8192]{1,0:T(8,128)}, u32[]{:S(2)}) copy-start(f32[40,8192]{1,0:T(8,128)} %get-tuple-element.8) | copy-start | bytes 3932164
  101.2 45.0 %copy-start.3 = (f32[1,40,8192]{2,1,0:T(8,128)S(1)}, f32[1,40,8192]{2,1,0:T(8,128)}, u32[]{:S(2)}) copy-start(f32[1,40,8192]{2,1,0:T(8,128)} %param.10) | copy-start | bytes 3932164

commit v3 on v2

--- a/solution.py
+++ b/solution.py
@@ -27,51 +27,85 @@
     )
 
 
-def doubling_kernel(bits, x_ref, o_ref, held, landed, send_sem, recv_sem):
+def sum_kernel(rounds, split, x_ref, o_ref, held, landed, across, send_sem, recv_sem, side_send, side_recv):
     field = lax.axis_index("field")
     dom = lax.axis_index("dom")
-    partners = [(1 - field, dom)]
-    for bit in range(bits):
-        step = 1 << bit
-        partners.append((field, dom + (1 - 2 * ((dom // step) % 2)) * step))
+    groups = []
+    for step, members in rounds:
+        low = (1 - 2 * ((dom // step) % 2)) * step
+        high = (1 - 2 * ((dom // (2 * step)) % 2)) * 2 * step
+        groups.append([dom + (e % 2) * low + (e // 2) * high for e in range(1, members)])
     barrier = pltpu.get_barrier_semaphore()
-    for partner in partners:
-        pl.semaphore_signal(
-            barrier, inc=1, device_id=partner, device_id_type=pl.DeviceIdType.MESH
-        )
-    held[0] = x_ref[...]
-    pl.semaphore_wait(barrier, len(partners))
-    for step, partner in enumerate(partners):
+    peers = [(1 - field, dom)] + [(field, peer) for group in groups for peer in group]
+    for peer in peers:
+        pl.semaphore_signal(barrier, inc=1, device_id=peer, device_id_type=pl.DeviceIdType.MESH)
+    pl.semaphore_wait(barrier, len(peers))
+
+    def send(source, target, sems, peer):
         copy = pltpu.make_async_remote_copy(
-            src_ref=held.at[step],
-            dst_ref=landed.at[step],
-            send_sem=send_sem.at[step],
-            recv_sem=recv_sem.at[step],
-            device_id=partner,
+            src_ref=source,
+            dst_ref=target,
+            send_sem=sems[0],
+            recv_sem=sems[1],
+            device_id=peer,
             device_id_type=pl.DeviceIdType.MESH,
         )
         copy.start()
+        return copy
+
+    mine, theirs = (field, 1 - field) if split else (0, 0)
+    copy = send(
+        x_ref.at[theirs], across.at[0], (side_send.at[0], side_recv.at[0]), (1 - field, dom)
+    )
+    copy.wait()
+    total = x_ref[mine] + across[0]
+    for turn, group in enumerate(groups):
+        held[turn] = total
+        copies = [
+            send(
+                held.at[turn],
+                landed.at[turn, e],
+                (send_sem.at[turn, e], recv_sem.at[turn, e]),
+                (field, peer),
+            )
+            for e, peer in enumerate(group)
+        ]
+        for copy in copies:
+            copy.wait()
+        total = total + landed[turn, 0]
+        if len(group) == 3:
+            total = total + (landed[turn, 1] + landed[turn, 2])
+    o_ref[mine] = total
+    if split:
+        held[len(groups)] = total
+        copy = send(
+            held.at[len(groups)],
+            across.at[1],
+            (side_send.at[1], side_recv.at[1]),
+            (1 - field, dom),
+        )
         copy.wait()
-        total = held[step] + landed[step]
-        if step + 1 < len(partners):
-            held[step + 1] = total
-        else:
-            o_ref[...] = total
+        o_ref[theirs] = across[1]
 
 
 def summed_everywhere(x, collective_id):
     bits = (lax.axis_size("dom") - 1).bit_length()
-    steps = bits + 1
+    rounds = [(1 << bit, 4 if bit + 1 < bits else 2) for bit in range(0, bits, 2)]
+    cell = x.shape[1:]
+    slots = len(rounds)
     return pl.pallas_call(
-        functools.partial(doubling_kernel, bits),
+        functools.partial(sum_kernel, rounds, x.shape[0] == 2),
         out_shape=jax.ShapeDtypeStruct(x.shape, x.dtype),
         in_specs=[pl.BlockSpec(memory_space=pltpu.VMEM)],
         out_specs=pl.BlockSpec(memory_space=pltpu.VMEM),
         scratch_shapes=[
-            pltpu.VMEM((steps,) + x.shape, x.dtype),
-            pltpu.VMEM((steps,) + x.shape, x.dtype),
-            pltpu.SemaphoreType.DMA((steps,)),
-            pltpu.SemaphoreType.DMA((steps,)),
+            pltpu.VMEM((slots + 1,) + cell, x.dtype),
+            pltpu.VMEM((slots, 3) + cell, x.dtype),
+            pltpu.VMEM((2,) + cell, x.dtype),
+            pltpu.SemaphoreType.DMA((slots, 3)),
+            pltpu.SemaphoreType.DMA((slots, 3)),
+            pltpu.SemaphoreType.DMA((2,)),
+            pltpu.SemaphoreType.DMA((2,)),
         ],
         compiler_params=pltpu.CompilerParams(
             collective_id=collective_id, has_side_effects=True
@@ -101,7 +135,7 @@
         rows_out[span, :] = jnp.zeros((LANES, LANES), jnp.float32)
         return carry
 
-    lax.fori_loop(0, wide // LANES, turn_in, 0, unroll=2)
+    lax.fori_loop(0, wide // LANES, turn_in, 0, unroll=16)
 
     def term(n, shift, offset, at, dims):
         block = window[:, pl.ds(pl.multiple_of((n + 2 + shift) * BS, BS), BS)]
@@ -130,7 +164,7 @@
         o_ref[:, span] = o_ref[:, span] + rows_out[span, :].T[:columns]
         return carry
 
-    lax.fori_loop(0, wide // LANES, turn_out, 0, unroll=2)
+    lax.fori_loop(0, wide // LANES, turn_out, 0, unroll=16)
 
 
 def operate(vectors, kinds, scales, tables, places, weights):
@@ -182,7 +216,7 @@
     partial_sums = jnp.stack(
         [jnp.sum(vec_modes * vec_modes, axis=1), jnp.sum(vec_modes * image_x, axis=1)]
     )
-    sums = summed_everywhere(jnp.pad(partial_sums, ((0, 6), (0, 128 - columns))), 1)
+    sums = summed_everywhere(jnp.pad(partial_sums, ((0, 6), (0, LANES - columns)))[None], 1)[0]
     quotient = sums[1, :columns] / sums[0, :columns]
     eye = jnp.eye(BS, dtype=jnp.bool_)
     diag_table = jnp.sum(
@@ -210,7 +244,9 @@
         jnp.pad(part_b, ((0, 0), (0, 8))),
         jnp.pad(part_a, ((0, 0), (1, 7))),
     )
-    packed = summed_everywhere(packed, 2)
+    half = -(-size // 16) * 8
+    packed = jnp.pad(packed, ((0, 2 * half - size), (0, 0))).reshape(2, half, size + 8)
+    packed = summed_everywhere(packed, 2).reshape(2 * half, size + 8)[:size]
     low = jnp.where(col <= row, packed, 0.0)[:, :size]
     high_part = packed[:, 1 : size + 1]
     square_row, square_col = row[:, :size], col[:, :size]

time: 155 us -> 139 us (0.90)
  Pallas kernels: 85.4 us -> 68.6 us
    pallas_call x2, Pallas kernels: 37.9 us -> 29 us  [summed_everywhere(): pl.pallas_call(functools.partial(sum_kernel, rounds, x.shape[0] == 2), ou...]
    pallas_call x2, Pallas kernels: 47.5 us -> 39.7 us  [operate(): pl.pallas_call(operator_kernel, out_shape=jax.ShapeDtypeStruct((columns,...]
  transfers between devices with their start and end apart: 7 -> 7, of which waited for: 2 -> 2; matrix products, arithmetic and copies ran while one was open for 7% -> 8% of each run, Pallas kernels for 0% -> 0%
where the time goes in v3:
time: 139 us; the launch traced here: 138 us
  Pallas kernels  68.6 us (49%)
  other arithmetic  34.6 us (25%)
  matrix products  14 us (10%)
  starting transfers between devices  11.4 us (8%)
  local copies, waits for them, and re-layouts  4.82 us (3%)
  waiting for transfers between devices  2.74 us (2%)
  between operations  1.85 us (1%)
    pallas_call x2, Pallas kernels, operate(): pl.pallas_call(operator_kernel, out_shape=jax.ShapeDtypeStruct((columns,...  39.7 us
    pallas_call x2, Pallas kernels, summed_everywhere(): pl.pallas_call(functools.partial(sum_kernel, rounds, x.shape[0] == 2), ou...  29 us
    another operation x3, other arithmetic, shards(): chol = jnp.linalg.cholesky(gram_b, symmetrize_input=False)  11.6 us
    another operation x2, other arithmetic, shards(): basis = jax.scipy.linalg.solve_triangular(chol, search, lower=True)  9.85 us
    ppermute x2, starting transfers between devices, halos(): lax.ppermute(tail, axis, [(i, i + 1) for i in range(ends)])  8 us
    another operation x1, matrix products, shards(): basis = jax.scipy.linalg.solve_triangular(chol, search, lower=True)  6.74 us
    convert_element_type x2, other arithmetic, operate(): rounded = vectors.astype(jnp.bfloat16)  5.18 us
    dot_general x1, matrix products, shards(): part_b = jnp.dot(search, search.T, precision=high)  4.2 us
  transfers between devices with their start and end apart: 7, of which 2 were waited for; matrix products, arithmetic and copies ran while one was open for 8% of the time, Pallas kernels for 0%

profile of v3, /device:TPU:0, one launch (start us, length us, event | category | flops | bytes accessed | tf_op | source)
XLA Modules:
  0.0 138.1 jit_solution(14779984837490329827)
XLA Ops:
  0.7 3.1 %fusion.27 = bf16[80,8192]{1,0:T(8,128)(2,1)} fusion(f32[40,8192]{1,0:T(8,128)} %bitcast.85, f32[40,8192]{1,0:T(8,128)} %bitcast.80), kind=kLoop, calls=%fused_computation.65 | loop fusion | flops 2621440 | bytes 3932160 | tf_op jit(solution)/shard_map/convert_element_type | solution.py:172
  3.7 0.5 collective-permute-start.3
  4.2 1.7 %fusion.29 = (bf16[80,1024]{1,0:T(8,128)(2,1)}, bf16[80,1024]{1,0:T(8,128)(2,1)}) fusion(bf16[80,8192]{1,0:T(8,128)(2,1)} %fusion.27), kind=kLoop, calls=%fused_computation.67 | loop fusion | bytes 655360 | tf_op jit(solution)/shard_map/slice | solution.py:22
  6.0 5.0 %collective-permute-start.1 = (bf16[80,1024]{1,0:T(8,128)(2,1)}, bf16[80,1024]{1,0:T(8,128)(2,1)}, u32[]{:S(2)}, u32[]{:S(2)}) collective-permute-start(bf16[80,1024]{1,0:T(8,128)(2,1)} %get-tuple-element.10), channel_id=1, source_target_pairs={{0,1},{1,2},{2,3},{3,4},{4,5},{5,6},{6,7},{7,8},{8,9},{9,10},{10,1... | collective-permute-start | bytes 491528 | tf_op jit(solution)/shard_map/ppermute | solution.py:25
  11.0 1.3 collective-permute-start.2
  12.6 0.8 iota_compare_fusion
  14.4 2.2 %fusion = f32[4,512]{1,0:T(4,128)S(1)} fusion(bf16[1,3,4,512,512]{4,3,2,1,0:T(8,128)(2,1)} %param.14, pred[512,512]{1,0:T(8,128)(4,1)} %iota_compare_fusion), kind=kLoop, calls=%fused_computation.2 | loop fusion | flops 3143680 | bytes 2367488 | tf_op jit(solution)/shard_map/reduce_sum | solution.py:222
  16.8 1.5 %pad_maximum_fusion.1.x_ref = f32[80,8192]{1,0:T(8,128)S(1)} fusion(f32[40,8192]{1,0:T(8,128)} %bitcast.86, f32[40,8192]{1,0:T(8,128)S(1)} %bitcast.82), kind=kLoop, calls=%fused_computation.10 | loop fusion | flops 655360 | bytes 5242880 | tf_op jit(solution)/shard_map/concatenate | solution.py:213
  18.4 1.8 %collective-permute-done.2.after = bf16[80,1024]{1,0:T(8,128)(2,1)} collective-permute-done((bf16[80,1024]{1,0:T(8,128)(2,1)}, bf16[80,1024]{1,0:T(8,128)(2,1)}, u32[]{:S(2)}, u32[]{:S(2)}) %collective-permute-start.2) | collective-permute-done | bytes 163872 | tf_op jit(solution)/shard_map/ppermute | solution.py:26
  20.3 19.9 %shard_map.95 = f32[80,8192]{1,0:T(8,128)S(1)} custom-call(s32[3,18]{1,0:T(4,128)S(1)} %pad_dynamic-slice_fusion.1.kinds, f32[3,18]{1,0:T(4,128)S(1)} %pad_dynamic-slice_fusion.scales, s32[3072]{0:T(1024)S(1)} %shift-left_or_fusion.places, f32[3072]{0:T(1024)S(1)} %fusion.18.weights, f32[80,8192]{1,0:T(8,128)S(1)} %pad_maximum_fusion.1.x_ref, ...), custom_call_target="tpu_custom_call" | custom-call | flops 3355443200 | bytes 10485760 | tf_op jit(solution)/shard_map/pallas_call | solution.py:177
  40.2 1.8 %multiply_reduce_fusion.1 = (f32[40]{0:T(128)S(1)}, f32[40]{0:T(128)S(1)}, f32[40,8192]{1,0:T(8,128)}, f32[40,8192]{1,0:T(8,128)}) fusion(f32[1,40,8192]{2,1,0:T(8,128)S(1)} %copy-done.1, f32[80,8192]{1,0:T(8,128)S(1)} %shard_map.95), kind=kLoop, calls=%fused_computation.14 | loop fusion | flops 1310640 | bytes 6553920 | tf_op jit(solution)/shard_map/reduce_sum | solution.py:217
  42.0 0.7 copy-done
  42.7 0.6 fusion.19.x_ref
  43.3 12.5 %shard_map.96 = f32[1,8,128]{2,1,0:T(8,128)} custom-call(f32[1,8,128]{2,1,0:T(8,128)} %fusion.19.x_ref), custom_call_target="tpu_custom_call" | custom-call | tf_op jit(solution)/shard_map/pallas_call | solution.py:96
  55.8 0.8 fusion.20
  56.6 2.1 %fusion.28 = (bf16[40,8192]{1,0:T(8,128)(2,1)S(1)}, f32[40,8192]{1,0:T(8,128)S(1)}) fusion(f32[8192]{0:T(1024)S(1)} %bitcast.93, f32[40]{0:T(128)S(1)} %fusion.20, f32[1,40,8192]{2,1,0:T(8,128)} %param.10, f32[80,8192]{1,0:T(8,128)} %copy-done), kind=kLoop, calls=%fused_computation.66 | loop fusion | flops 1310720 | bytes 4620448 | tf_op jit(solution)/shard_map/convert_element_type | solution.py:172
  58.8 3.0 %collective-permute-start.4 = (bf16[40,1024]{1,0:T(8,128)(2,1)S(1)}, bf16[40,1024]{1,0:T(8,128)(2,1)S(1)}, u32[]{:S(2)}, u32[]{:S(2)}) collective-permute-start(bf16[40,1024]{1,0:T(8,128)(2,1)S(1)} %get-tuple-element.12), channel_id=1, source_target_pairs={{0,1},{1,2},{2,3},{3,4},{4,5},{5,6},{6,7},{7,8},{8,9},{9,10},{10,1... | collective-permute-start | bytes 245768 | tf_op jit(solution)/shard_map/ppermute | solution.py:25
  61.8 1.3 collective-permute-start.5
  63.1 4.2 %fusion.7 = f32[120,120]{0,1:T(8,128)S(1)} fusion(f32[40,8192]{1,0:T(8,128)} %bitcast.87, f32[40,8192]{1,0:T(8,128)S(1)} %get-tuple-element.6.x_ref, f32[40,8192]{1,0:T(8,128)} %bitcast.81), kind=kOutput, calls=%fused_computation.11 | convolution fusion | flops 709754880 | bytes 3989760 | tf_op jit(solution)/shard_map/dot_general | solution.py:236
  67.4 0.9 collective-permute-done.5.after
  68.3 19.7 %shard_map.97 = f32[40,8192]{1,0:T(8,128)S(1)} custom-call(s32[3,18]{1,0:T(4,128)S(1)} %pad_dynamic-slice_fusion.1.kinds, f32[3,18]{1,0:T(4,128)S(1)} %pad_dynamic-slice_fusion.scales, s32[3072]{0:T(1024)S(1)} %shift-left_or_fusion.places, f32[3072]{0:T(1024)S(1)} %fusion.18.weights, f32[40,8192]{1,0:T(8,128)S(1)} %get-tuple-element.6.x_ref, ...), custom_call_target="tpu_custom_call" | custom-call | flops 1677721600 | bytes 5242880 | tf_op jit(solution)/shard_map/pallas_call | solution.py:177
  88.1 1.8 %fusion.1 = f32[120,120]{1,0:T(8,128)S(1)} fusion(f32[40,8192]{1,0:T(8,128)S(1)} %copy-done.6, f32[40,8192]{1,0:T(8,128)S(1)} %shard_map.97, f32[40,8192]{1,0:T(8,128)S(1)} %copy-done.5, f32[40,8192]{1,0:T(8,128)S(1)} %bitcast.89, f32[40,8192]{1,0:T(8,128)S(1)} %get-tuple-element.6.x_ref, f32[40,8192]{1,0:T(8,128)S(1)} %bitcast.83), kind=kOutput, calls=%fused_computation.4 | convolution fusion | flops 711720960 | bytes 7921920 | tf_op jit(solution)/shard_map/dot_general | solution.py:237
  90.1 0.6 pad.29.clone
  90.7 16.5 %shard_map.98 = f32[2,64,128]{2,1,0:T(8,128)} custom-call(f32[2,64,128]{2,1,0:T(8,128)} %bitcast.92), custom_call_target="tpu_custom_call" | custom-call | tf_op jit(solution)/shard_map/pallas_call | solution.py:96
  107.2 1.0 fusion.31
  108.4 11.0 %cholesky.16 = f32[120,120]{1,0:T(8,128)S(1)} custom-call(f32[120,120]{1,0:T(8,128)S(1)} %fusion.15), custom_call_target="Cholesky" | custom-call | tf_op jit(solution)/shard_map/jit(cholesky)/cholesky | solution.py:255
  119.5 0.6 compare_reduce_fusion
  120.1 0.7 fusion.8
  120.8 9.2 %custom-call.10 = f32[1,120,120]{1,2,0:T(8,128)S(1)} custom-call(f32[1,120,120]{2,1,0:T(8,128)S(1)} %fusion.8), custom_call_target="InvertDiagBlocksLowerTriangular" | custom-call | tf_op jit(solution)/shard_map/jit(_solve_triangular)/triangular_solve | solution.py:258
  130.1 6.7 %convolution_bitcast_fusion = f32[1,120,8192]{2,1,0:T(8,128)} fusion(f32[40,8192]{1,0:T(8,128)} %bitcast.88, f32[40,8192]{1,0:T(8,128)S(1)} %get-tuple-element.6.x_ref, f32[40,8192]{1,0:T(8,128)S(1)} %bitcast.84, f32[1,120,120]{1,2,0:T(8,128)S(1)} %custom-call.10), kind=kOutput, calls=%fused_computation | convolution fusion | flops 1417543680 | bytes 7921920 | tf_op jit(solution)/shard_map/jit(_solve_triangular)/triangular_solve | solution.py:258
  136.8 0.3 convolution_bitcast_fusion.1
  137.2 0.9 fusion.12
  (63 shorter events, 1.4 us)
Async XLA Ops:
  0.6 11.7 %copy-start.9 = (s32[1,3072]{1,0:T(1,128)S(1)}, s32[1,3072]{1,0:T(1,128)}, u32[]{:S(2)}) copy-start(s32[1,3072]{1,0:T(1,128)} %param.15) | copy-start | bytes 36868
  0.6 12.7 %copy-start.10 = (f32[1,3,256]{2,0,1:T(1,128)S(1)}, f32[1,3,256]{2,0,1:T(1,128)}, u32[]{:S(2)}) copy-start(f32[1,3,256]{2,0,1:T(1,128)} %param.13) | copy-start | bytes 9220
  0.7 12.7 %copy-start.11 = (s32[1,3,256]{2,0,1:T(1,128)S(1)}, s32[1,3,256]{2,0,1:T(1,128)}, u32[]{:S(2)}) copy-start(s32[1,3,256]{2,0,1:T(1,128)} %param.12) | copy-start | bytes 9220
  0.7 19.6 %slice-start = ((s8[6291456]{0:T(1024)(128)(4,1)}), s8[2097152]{0:T(1024)(128)(4,1)S(1)}, s32[]{:S(2)}) async-start(s8[6291456]{0:T(1024)(128)(4,1)} %bitcast.74), calls=%async_computation | async-start | bytes 4194304
  3.7 16.5 %collective-permute-start.3 = (bf16[80,8192]{1,0:T(8,128)(2,1)}, bf16[80,8192]{1,0:T(8,128)(2,1)S(1)}, u32[]{:S(2)}, u32[]{:S(2)}) collective-permute-start(bf16[80,8192]{1,0:T(8,128)(2,1)} %fusion.27), channel_id=1, source_target_pairs={{0,16},{16,0},{1,17},{17,1},{2,18},{18,2},{3,19},{19,3},{4,20},{20... | collective-permute-start | bytes 3932168 | tf_op jit(solution)/shard_map/ppermute | solution.py:16
  6.0 12.4 %collective-permute-start.1 = (bf16[80,1024]{1,0:T(8,128)(2,1)}, bf16[80,1024]{1,0:T(8,128)(2,1)}, u32[]{:S(2)}, u32[]{:S(2)}) collective-permute-start(bf16[80,1024]{1,0:T(8,128)(2,1)} %get-tuple-element.10), channel_id=1, source_target_pairs={{0,1},{1,2},{2,3},{3,4},{4,5},{5,6},{6,7},{7,8},{8,9},{9,10},{10,1... | collective-permute-start | bytes 491528 | tf_op jit(solution)/shard_map/ppermute | solution.py:25
  11.0 9.2 %collective-permute-start.2 = (bf16[80,1024]{1,0:T(8,128)(2,1)}, bf16[80,1024]{1,0:T(8,128)(2,1)}, u32[]{:S(2)}, u32[]{:S(2)}) collective-permute-start(bf16[80,1024]{1,0:T(8,128)(2,1)} %get-tuple-element.9), channel_id=1, source_target_pairs={{1,0},{2,1},{3,2},{4,3},{5,4},{6,5},{7,6},{8,7},{9,8},{10,9},{11,1... | collective-permute-start | bytes 491528 | tf_op jit(solution)/shard_map/ppermute | solution.py:26
  12.3 6.1 %collective-permute-start = (s32[3072]{0:T(1024)S(1)}, s32[3072]{0:T(1024)S(1)}, u32[]{:S(2)}, u32[]{:S(2)}) collective-permute-start(s32[3072]{0:T(1024)S(1)} %bitcast.96), channel_id=1, source_target_pairs={{0,16},{16,0},{1,17},{17,1},{2,18},{18,2},{3,19},{19,3},{4,20},{20... | collective-permute-start | bytes 36872 | tf_op jit(solution)/shard_map/ppermute | solution.py:16
  13.4 3.4 %copy-start.1 = (f32[1,40,8192]{2,1,0:T(8,128)S(1)}, f32[1,40,8192]{2,1,0:T(8,128)}, u32[]{:S(2)}) copy-start(f32[1,40,8192]{2,1,0:T(8,128)} %param.10) | copy-start | bytes 3932164
  14.4 5.8 %slice-start.1 = ((s8[6291456]{0:T(1024)(128)(4,1)}), s8[4194304]{0:T(1024)(128)(4,1)S(1)}, s32[]{:S(2)}) async-start(s8[6291456]{0:T(1024)(128)(4,1)} %bitcast.74), calls=%async_computation.1 | async-start | bytes 8388608
  16.8 1.5 %copy-start.8 = (f32[3072]{0:T(1024)S(1)}, f32[3072]{0:T(1024)}, u32[]{:S(2)}) copy-start(f32[3072]{0:T(1024)} %param.17) | copy-start | bytes 36868
  40.2 2.5 %copy-start = (f32[80,8192]{1,0:T(8,128)}, f32[80,8192]{1,0:T(8,128)S(1)}, u32[]{:S(2)}) copy-start(f32[80,8192]{1,0:T(8,128)S(1)} %shard_map.95) | copy-start | bytes 7864324
  40.2 28.1 %slice-start.2 = ((s8[6291456]{0:T(1024)(128)(4,1)}), s8[2097152]{0:T(1024)(128)(4,1)S(1)}, s32[]{:S(2)}) async-start(s8[6291456]{0:T(1024)(128)(4,1)} %bitcast.77), calls=%async_computation.2 | async-start | bytes 4194304
  56.6 11.7 %slice-start.3 = ((s8[6291456]{0:T(1024)(128)(4,1)}), s8[4194304]{0:T(1024)(128)(4,1)S(1)}, s32[]{:S(2)}) async-start(s8[6291456]{0:T(1024)(128)(4,1)} %bitcast.77), calls=%async_computation.3 | async-start | bytes 8388608
  58.7 9.6 %collective-permute-start.6 = (bf16[40,8192]{1,0:T(8,128)(2,1)S(1)}, bf16[40,8192]{1,0:T(8,128)(2,1)S(1)}, u32[]{:S(2)}, u32[]{:S(2)}) collective-permute-start(bf16[40,8192]{1,0:T(8,128)(2,1)S(1)} %get-tuple-element.5), channel_id=1, source_target_pairs={{0,16},{16,0},{1,17},{17,1},{2,18},{18,2},{3,19},{19,3},{4,20},{20... | collective-permute-start | bytes 1966088 | tf_op jit(solution)/shard_map/ppermute | solution.py:16
  58.8 8.5 %collective-permute-start.4 = (bf16[40,1024]{1,0:T(8,128)(2,1)S(1)}, bf16[40,1024]{1,0:T(8,128)(2,1)S(1)}, u32[]{:S(2)}, u32[]{:S(2)}) collective-permute-start(bf16[40,1024]{1,0:T(8,128)(2,1)S(1)} %get-tuple-element.12), channel_id=1, source_target_pairs={{0,1},{1,2},{2,3},{3,4},{4,5},{5,6},{6,7},{7,8},{8,9},{9,10},{10,1... | collective-permute-start | bytes 245768 | tf_op jit(solution)/shard_map/ppermute | solution.py:25
  61.8 6.5 %collective-permute-start.5 = (bf16[40,1024]{1,0:T(8,128)(2,1)S(1)}, bf16[40,1024]{1,0:T(8,128)(2,1)S(1)}, u32[]{:S(2)}, u32[]{:S(2)}) collective-permute-start(bf16[40,1024]{1,0:T(8,128)(2,1)S(1)} %get-tuple-element.11), channel_id=1, source_target_pairs={{1,0},{2,1},{3,2},{4,3},{5,4},{6,5},{7,6},{8,7},{9,8},{10,9},{11,1... | collective-permute-start | bytes 245768 | tf_op jit(solution)/shard_map/ppermute | solution.py:26
  67.3 20.7 %copy-start.2 = (f32[1,40,8192]{2,1,0:T(8,128)S(1)}, f32[1,40,8192]{2,1,0:T(8,128)}, u32[]{:S(2)}) copy-start(f32[1,40,8192]{2,1,0:T(8,128)} %param.10) | copy-start | bytes 3932164
  67.3 20.7 %copy-start.4 = (f32[1,40,8192]{2,1,0:T(8,128)S(1)}, f32[1,40,8192]{2,1,0:T(8,128)}, u32[]{:S(2)}) copy-start(f32[1,40,8192]{2,1,0:T(8,128)} %param.11) | copy-start | bytes 3932164
  67.3 20.7 %copy-start.5 = (f32[40,8192]{1,0:T(8,128)S(1)}, f32[40,8192]{1,0:T(8,128)}, u32[]{:S(2)}) copy-start(f32[40,8192]{1,0:T(8,128)} %get-tuple-element.7) | copy-start | bytes 3932164
  67.3 20.7 %copy-start.6 = (f32[40,8192]{1,0:T(8,128)S(1)}, f32[40,8192]{1,0:T(8,128)}, u32[]{:S(2)}) copy-start(f32[40,8192]{1,0:T(8,128)} %get-tuple-element.8) | copy-start | bytes 3932164
  89.9 40.2 %copy-start.3 = (f32[1,40,8192]{2,1,0:T(8,128)S(1)}, f32[1,40,8192]{2,1,0:T(8,128)}, u32[]{:S(2)}) copy-start(f32[1,40,8192]{2,1,0:T(8,128)} %param.10) | copy-start | bytes 3932164
  130.1 6.8 %copy-start.7 = (f32[2,64,128]{2,1,0:T(8,128)S(1)}, f32[2,64,128]{2,1,0:T(8,128)}, u32[]{:S(2)}) copy-start(f32[2,64,128]{2,1,0:T(8,128)} %shard_map.98) | copy-start | bytes 196612
